TPU v7x, 32 devices: a whole 2x2x4 slice. The times are simulated.
32 devices in a mesh: dp: 2 (over core), expert: 16 (over z, y, x).
Axes of the slice: x: 2, y: 2, z: 4, core: 2. Of those that a mesh axis runs over, the one named last changes fastest.
Arguments:
- tokens: bfloat16 [2048, 4096], P(('dp', 'expert')), parts along dimension 0, may hold values from -6 to 6
- expert_ids: int32 [2048, 2], P(('dp', 'expert')), parts along dimension 0, may hold values from 0 to 7, all different within a row; in each aligned block of 64 rows (0 to 63, 64 to 127, ...) at most 24 rows name the same one
- route_weights: float32 [2048, 2], P(('dp', 'expert')), parts along dimension 0, may hold values from 0.1 to 1
- norm_gain: float32 [4096], replicated, may hold values from 0.1 to 1.9
- w_gate: bfloat16 [16, 4096, 896], P('expert'), may hold values from -0.09375 to 0.09375
- w_up: bfloat16 [16, 4096, 896], P('expert'), may hold values from -0.09375 to 0.09375
- w_down: bfloat16 [16, 896, 4096], P('expert'), may hold values from -0.125 to 0.125
Outputs:
- layer_out: bfloat16 [2048, 4096], P(('dp', 'expert')), parts along dimension 0
There are 2 independent parts, one for each index of `dp`. A program takes and returns all parts, laid end to end along the dimension named above; an argument that names none is the same for every part. Nothing has to cross between parts.
Inputs may be any that keep to these rules, and one draw needn't show every extreme that they name: `expert_ids`: each token names two different experts; among the 64 tokens of one device no expert is named more than 24 times, a bound that some block reaches.
All inputs are finite; a program needn't handle non-finite values.
Results may differ from a plain program's by a relative error of at most 0.006.
Values may be sent and summed in bfloat16 or wider, within the bound.
No kernel may reach another device: no remote copies, remote signals or barrier semaphores. Data moves between devices by JAX's collectives and lax.ppermute only.
A program may use at most 128 MiB of HBM per device.

v0:
```python
import jax
import jax.numpy as jnp
from jax import lax
from jax.sharding import PartitionSpec as P

EXPERTS = 8
CAP = 24


def rms_norm(values, norm_gain):
    wide = values.astype(jnp.float32)
    mean_square = jnp.mean(wide * wide, axis=-1, keepdims=True)
    return (wide * lax.rsqrt(mean_square + 1e-05) * norm_gain).astype(jnp.bfloat16)


def body(tokens, expert_ids, route_weights, norm_gain, w_gate, w_up, w_down):
    n_devices = lax.axis_size("expert")
    shards = n_devices // EXPERTS
    tok_count = tokens.shape[0]
    width_model = tokens.shape[1]
    normed = rms_norm(tokens, norm_gain)
    flat_ids = expert_ids.reshape(tok_count * 2)
    onehot = (flat_ids[:, None] == jnp.arange(EXPERTS, dtype=jnp.int32)[None, :]).astype(jnp.int32)
    rank_in = jnp.sum((jnp.cumsum(onehot, axis=0) - onehot) * onehot, axis=1)
    slot_index = (flat_ids * CAP + rank_in).reshape(tok_count, 2)
    columns = jnp.arange(EXPERTS * CAP, dtype=jnp.int32)
    hits = slot_index[:, :, None] == columns[None, None, :]
    selector = jnp.any(hits, axis=1).T.astype(jnp.bfloat16)
    weight_table = jnp.sum(jnp.where(hits, route_weights[:, :, None], 0.0), axis=1)
    slots = jnp.dot(selector, normed, preferred_element_type=jnp.float32).astype(jnp.bfloat16)
    slots = slots.reshape(EXPERTS, CAP, width_model)
    outgoing = jnp.broadcast_to(slots[:, None], (EXPERTS, shards, CAP, width_model))
    outgoing = outgoing.reshape(n_devices, CAP, width_model)
    arrived = lax.all_to_all(outgoing, "expert", split_axis=0, concat_axis=0, tiled=True)
    count_items = arrived.shape[1]
    row_block = arrived.reshape(n_devices * count_items, width_model)
    gate_act = jnp.dot(row_block, w_gate[0], preferred_element_type=jnp.float32)
    up_act = jnp.dot(row_block, w_up[0], preferred_element_type=jnp.float32)
    hidden = (jax.nn.silu(gate_act) * up_act).astype(jnp.bfloat16)
    expert_out = jnp.dot(hidden, w_down[0], preferred_element_type=jnp.float32)
    partial_value = expert_out.reshape(n_devices, count_items, width_model)
    returned = lax.all_to_all(partial_value, "expert", split_axis=0, concat_axis=0, tiled=True)
    combined = jnp.sum(returned.reshape(EXPERTS, shards, CAP, width_model), axis=1)
    mixture = jnp.dot(
        weight_table,
        combined.reshape(EXPERTS * CAP, width_model),
        precision=lax.Precision.HIGHEST,
        preferred_element_type=jnp.float32,
    )
    return (tokens.astype(jnp.float32) + mixture).astype(jnp.bfloat16)


def solution(mesh):
    in_specs = (
        P(("dp", "expert"), None),
        P(("dp", "expert"), None),
        P(("dp", "expert"), None),
        P(),
        P("expert", None, None),
        P("expert", None, None),
        P("expert", None, None),
    )
    out_specs = P(("dp", "expert"), None)
    return jax.shard_map(body, mesh=mesh, in_specs=in_specs, out_specs=out_specs, check_vma=False)
```

profile of v0, /device:TPU:14, one launch (start us, length us, event | category | flops | bytes accessed | tf_op | source)
XLA Modules:
  0.0 246.3 jit_solution(1612698089558539943)
XLA Ops:
  0.0 0.8 copy.20
  0.8 0.1 eq.28
  0.9 0.1 fusion.20
  1.0 0.2 reduce_window_sum.11
  1.2 0.2 select_reduce_fusion.1
  1.4 0.1 reduce_sum.39
  1.5 0.1 copy.21
  1.6 0.7 multiply_add_fusion
  2.3 0.1 fusion.19
  2.4 0.0 slice-start
  2.4 1.4 fusion.13
  3.8 1.7 convolution_convert_fusion
  5.5 0.0 slice-start.1
  5.5 0.4 broadcast_in_dim.27
  5.9 0.0 slice-start.2
  5.9 0.0 slice-start.4
  5.9 76.4 %all_to_all.10 = bf16[16,24,4096]{2,1,0:T(8,128)(2,1)S(1)} all-to-all(bf16[16,24,4096]{2,1,0:T(8,128)(2,1)S(1)} %bitcast.27), channel_id=1, replica_groups=mesh['dp'=2,'expert'=16] {'expert'}, dimensions={0} | all-to-all | bytes 6291456 | tf_op jit(solution)/shard_map/all_to_all | solution.py:34
  82.3 0.0 slice-done
  82.3 0.0 slice-done.1
  82.3 0.0 slice-start.3
  82.3 0.0 slice-start.5
  82.3 3.4 %fusion.4 = f32[384,896]{1,0:T(8,128)S(1)} fusion(bf16[384,4096]{1,0:T(8,128)(2,1)S(1)} %bitcast.30, bf16[1,4096,896]{2,1,0:T(8,128)(2,1)S(1)} %bitcast.33), kind=kOutput, calls=%fused_computation.4 | convolution fusion | flops 2818572288 | bytes 11862016 | tf_op jit(solution)/shard_map/dot_general | solution.py:37
  85.7 0.0 slice-done.2
  85.7 0.0 slice-done.3
  85.8 3.4 %fusion.10 = bf16[384,896]{1,0:T(8,128)(2,1)S(1)} fusion(bf16[384,4096]{1,0:T(8,128)(2,1)S(1)} %bitcast.31, bf16[1,4096,896]{2,1,0:T(8,128)(2,1)S(1)} %bitcast.35, f32[384,896]{1,0:T(8,128)S(1)} %fusion.4), kind=kOutput, calls=%fused_computation.13 | convolution fusion | flops 2820636672 | bytes 12550144 | tf_op jit(solution)/shard_map/dot_general | solution.py:38
  89.2 0.0 slice-done.4
  89.2 0.0 slice-done.5
  89.2 5.3 %fusion = f32[16,24,4096]{2,1,0:T(8,128)} fusion(bf16[16,24,896]{2,1,0:T(8,128)(2,1)S(1)} %bitcast.38, bf16[1,896,4096]{2,1,0:T(8,128)(2,1)S(1)} %bitcast.37), kind=kOutput, calls=%fused_computation | convolution fusion | flops 2818572288 | bytes 14319616 | tf_op jit(solution)/shard_map/dot_general | solution.py:40
  94.5 0.0 copy-start.1
  94.5 6.7 %all-to-all-start.1 = ((f32[16,24,4096]{2,1,0:T(8,128)}), f32[16,24,4096]{2,1,0:T(8,128)}, u32[]{:S(2)}, u32[]{:S(2)}) async-start(f32[16,24,4096]{2,1,0:T(8,128)} %fusion), calls=%async_computation.1 | async-start | bytes 12582912 | tf_op jit(solution)/shard_map/all_to_all | solution.py:42
  101.2 0.0 copy-done.1
  101.2 0.1 select_reduce_fusion
  101.3 0.0 copy-start
  101.3 138.4 %all-to-all-done.1 = f32[16,24,4096]{2,1,0:T(8,128)} async-done(((f32[16,24,4096]{2,1,0:T(8,128)}), f32[16,24,4096]{2,1,0:T(8,128)}, u32[]{:S(2)}, u32[]{:S(2)}) %all-to-all-start.1) | async-done | bytes 6291488 | tf_op jit(solution)/shard_map/all_to_all | solution.py:42
  239.7 3.7 %bitcast_reduce_fusion = f32[8,24,4096]{2,1,0:T(8,128)S(1)} fusion(f32[16,24,4096]{2,1,0:T(8,128)} %all-to-all-done.1), kind=kLoop, calls=%fused_computation.6 | loop fusion | flops 786432 | bytes 9437184 | tf_op jit(solution)/shard_map/reduce_sum | solution.py:43
  243.4 0.0 copy-done
  243.4 2.8 %fusion.6 = bf16[64,4096]{1,0:T(8,128)(2,1)} fusion(f32[64,192]{1,0:T(8,128)S(1)} %select_reduce_fusion, f32[192,4096]{1,0:T(8,128)S(1)} %bitcast.28, bf16[64,4096]{1,0:T(8,128)(2,1)S(1)} %copy-done), kind=kOutput, calls=%fused_computation.9 | convolution fusion | flops 604766208 | bytes 4243456 | tf_op jit(solution)/shard_map/dot_general | solution.py:44
  (4 shorter events, 0.0 us)
Async XLA Ops:
  2.4 79.9 %slice-start = ((s8[7340032]{0:T(1024)(128)(4,1)}), s8[4194304]{0:T(1024)(128)(4,1)S(1)}, s32[]{:S(2)}) async-start(s8[7340032]{0:T(1024)(128)(4,1)} %bitcast.32), calls=%async_computation.2 | async-start | bytes 8388608
  5.5 76.8 %slice-start.1 = ((s8[7340032]{0:T(1024)(128)(4,1)}), s8[3145728]{0:T(1024)(128)(4,1)S(1)}, s32[]{:S(2)}) async-start(s8[7340032]{0:T(1024)(128)(4,1)} %bitcast.32), calls=%async_computation.3 | async-start | bytes 6291456
  5.9 79.9 %slice-start.2 = ((s8[7340032]{0:T(1024)(128)(4,1)}), s8[4194304]{0:T(1024)(128)(4,1)S(1)}, s32[]{:S(2)}) async-start(s8[7340032]{0:T(1024)(128)(4,1)} %bitcast.34), calls=%async_computation.4 | async-start | bytes 8388608
  5.9 83.3 %slice-start.4 = ((s8[7340032]{0:T(1024)(128)(4,1)}), s8[4194304]{0:T(1024)(128)(4,1)S(1)}, s32[]{:S(2)}) async-start(s8[7340032]{0:T(1024)(128)(4,1)} %bitcast.36), calls=%async_computation.6 | async-start | bytes 8388608
  82.3 3.4 %slice-start.3 = ((s8[7340032]{0:T(1024)(128)(4,1)}), s8[3145728]{0:T(1024)(128)(4,1)S(1)}, s32[]{:S(2)}) async-start(s8[7340032]{0:T(1024)(128)(4,1)} %bitcast.34), calls=%async_computation.5 | async-start | bytes 6291456
  82.3 6.9 %slice-start.5 = ((s8[7340032]{0:T(1024)(128)(4,1)}), s8[3145728]{0:T(1024)(128)(4,1)S(1)}, s32[]{:S(2)}) async-start(s8[7340032]{0:T(1024)(128)(4,1)} %bitcast.36), calls=%async_computation.7 | async-start | bytes 6291456
  94.5 6.7 %copy-start.1 = (f32[64,2]{0,1:T(2,128)S(1)}, f32[64,2]{0,1:T(2,128)}, u32[]{:S(2)}) copy-start(f32[64,2]{0,1:T(2,128)} %param.9) | copy-start | bytes 1540
  94.5 145.2 %all-to-all-start.1 = ((f32[16,24,4096]{2,1,0:T(8,128)}), f32[16,24,4096]{2,1,0:T(8,128)}, u32[]{:S(2)}, u32[]{:S(2)}) async-start(f32[16,24,4096]{2,1,0:T(8,128)} %fusion), calls=%async_computation.1 | async-start | bytes 12582912 | tf_op jit(solution)/shard_map/all_to_all | solution.py:42
  101.3 142.1 %copy-start = (bf16[64,4096]{1,0:T(8,128)(2,1)S(1)}, bf16[64,4096]{1,0:T(8,128)(2,1)}, u32[]{:S(2)}) copy-start(bf16[64,4096]{1,0:T(8,128)(2,1)} %param.7) | copy-start | bytes 1572868
where the time goes:
time: 247 us; the launch traced here: 246 us
  waiting for transfers between devices  138 us (56%)
  blocking collectives  76.4 us (31%)
  matrix products  16.6 us (7%)
  starting transfers between devices  6.68 us (3%)
  other arithmetic  6.41 us (3%)
    all_to_all x1, waiting for transfers between devices, body(): lax.all_to_all(partial_value, 'expert', split_axis=0, concat_axis=0, tile...  138 us
    all_to_all x1, blocking collectives, body(): lax.all_to_all(outgoing, 'expert', split_axis=0, concat_axis=0, tiled=True)  76.4 us
    all_to_all x1, starting transfers between devices, body(): lax.all_to_all(partial_value, 'expert', split_axis=0, concat_axis=0, tile...  6.68 us
    dot_general x1, matrix products, body(): expert_out = jnp.dot(hidden, w_down[0], preferred_element_type=jnp.float32)  5.28 us
  transfers between devices with their start and end apart: 1, of which 1 were waited for; matrix products, arithmetic and copies ran while one was open for 0% of the time, Pallas kernels for 0%

commit v1 on v0

v1 whole, which is shorter than its diff:
```python
import jax
import jax.numpy as jnp
from jax import lax
from jax.sharding import PartitionSpec as P

EXPERTS = 8
CAP = 24
CHUNKS = 4


def rms_norm(values, norm_gain):
    wide = values.astype(jnp.float32)
    mean_square = jnp.mean(wide * wide, axis=-1, keepdims=True)
    return (wide * lax.rsqrt(mean_square + 1e-05) * norm_gain).astype(jnp.bfloat16)


def flip(values, mask, n_devices):
    if mask == 0:
        return values
    return lax.ppermute(values, "expert", [(i, i ^ mask) for i in range(n_devices)])


def body(tokens, expert_ids, route_weights, norm_gain, w_gate, w_up, w_down):
    n_devices = lax.axis_size("expert")
    shards = n_devices // EXPERTS
    tok_count, width = tokens.shape
    own_expert = lax.axis_index("expert") // shards
    normed = rms_norm(tokens, norm_gain)

    flat_ids = jnp.bitwise_xor(expert_ids, own_expert).reshape(tok_count * 2)
    onehot = (flat_ids[:, None] == jnp.arange(EXPERTS, dtype=jnp.int32)[None, :]).astype(jnp.int32)
    rank_in = jnp.sum((jnp.cumsum(onehot, axis=0) - onehot) * onehot, axis=1)
    slot_index = (flat_ids * CAP + rank_in).reshape(tok_count, 2)
    columns = jnp.arange(EXPERTS * CAP, dtype=jnp.int32)
    hits = slot_index[:, :, None] == columns[None, None, :]
    selector = jnp.any(hits, axis=1).T.astype(jnp.bfloat16)
    slots = jnp.dot(selector, normed, preferred_element_type=jnp.float32).astype(jnp.bfloat16)
    slots = slots.reshape(EXPERTS, CAP, width)
    picker = hits.transpose(1, 0, 2).reshape(2 * tok_count, EXPERTS, CAP).astype(jnp.bfloat16)
    weights = route_weights.T.reshape(2 * tok_count, 1)

    per = EXPERTS // CHUNKS
    mine = []
    for c in range(CHUNKS):
        blocks = [flip(slots[r], r * shards, n_devices) for r in range(c * per, (c + 1) * per)]
        mine.append(jnp.concatenate(blocks, axis=0))
    rows = per * CAP
    total = tokens.astype(jnp.float32)
    for c in range(CHUNKS):
        group = [flip(mine[c], m, n_devices) for m in range(shards)]
        row_block = jnp.concatenate(group, axis=0)
        gate_act = jnp.dot(row_block, w_gate[0], preferred_element_type=jnp.float32)
        up_act = jnp.dot(row_block, w_up[0], preferred_element_type=jnp.float32)
        hidden = (jax.nn.silu(gate_act) * up_act).astype(jnp.bfloat16)
        part = jnp.dot(hidden, w_down[0], preferred_element_type=jnp.float32)
        part = part.reshape(shards, rows, width)
        summed = part[0]
        for m in range(1, shards):
            summed = summed + flip(part[m].astype(jnp.bfloat16), m, n_devices).astype(jnp.float32)
        done = summed.astype(jnp.bfloat16).reshape(per, CAP, width)
        back = [flip(done[k], (c * per + k) * shards, n_devices) for k in range(per)]
        back = jnp.concatenate(back, axis=0)
        chosen = picker[:, c * per:(c + 1) * per].reshape(2 * tok_count, rows)
        picked = jnp.dot(chosen, back, preferred_element_type=jnp.float32)
        picked = (picked * weights).reshape(2, tok_count, width)
        total = total + picked[0] + picked[1]
    return total.astype(jnp.bfloat16)


def solution(mesh):
    in_specs = (
        P(("dp", "expert"), None),
        P(("dp", "expert"), None),
        P(("dp", "expert"), None),
        P(),
        P("expert", None, None),
        P("expert", None, None),
        P("expert", None, None),
    )
    out_specs = P(("dp", "expert"), None)
    return jax.shard_map(body, mesh=mesh, in_specs=in_specs, out_specs=out_specs, check_vma=False)
```

time: 247 us -> 182 us (0.74)
  the two profiles are of different devices: /device:TPU:14 before, /device:TPU:0 now
where the time goes in v1:
time: 182 us; the launch traced here: 181 us
  matrix products  55.8 us (31%)
  waiting for transfers between devices  53.2 us (29%)
  starting transfers between devices  52.3 us (29%)
  local copies, waits for them, and re-layouts  11.1 us (6%)
  other arithmetic  8.09 us (4%)
    ppermute x22, waiting for transfers between devices, flip(): lax.ppermute(values, 'expert', [(i, i ^ mask) for i in range(n_devices)])  53.2 us
    ppermute x22, starting transfers between devices, flip(): lax.ppermute(values, 'expert', [(i, i ^ mask) for i in range(n_devices)])  52.3 us
    dot_general x4, matrix products, body(): part = jnp.dot(hidden, w_down[0], preferred_element_type=jnp.float32)  35 us
    dot_general x3, matrix products, body(): up_act = jnp.dot(row_block, w_up[0], preferred_element_type=jnp.float32)  12.9 us
    slice x4, local copies, waits for them, and re-layouts, body(): part[m].astype(jnp.bfloat16)  5.18 us
    dot_general x1, matrix products, body(): gate_act = jnp.dot(row_block, w_gate[0], preferred_element_type=jnp.float32)  4.29 us
  transfers between devices with their start and end apart: 22, of which 7 were waited for; matrix products, arithmetic and copies ran while one was open for 38% of the time, Pallas kernels for 0%

profile of v1, /device:TPU:0, one launch (start us, length us, event | category | flops | bytes accessed | tf_op | source)
XLA Modules:
  0.0 180.9 jit_solution(10876649313329892804)
XLA Ops:
  0.0 1.2 fusion.24
  1.3 0.8 copy.12
  3.0 1.7 convolution_convert_fusion
  4.8 6.1 %collective-permute-start.17 = (bf16[24,4096]{1,0:T(8,128)(2,1)S(1)}, bf16[24,4096]{1,0:T(8,128)(2,1)S(1)}, u32[]{:S(2)}, u32[]{:S(2)}) collective-permute-start(bf16[24,4096]{1,0:T(8,128)(2,1)S(1)} %get-tuple-element.6), channel_id=1, source_target_pairs={{0,14},{1,15},{2,12},{3,13},{4,10},{5,11},{6,8},{7,9},{8,6},{9,7},... | collective-permute-start | bytes 589832 | tf_op jit(solution)/shard_map/ppermute | solution.py:20
  11.1 0.7 collective-permute-start.11
  11.8 2.0 %collective-permute-start.10 = (bf16[24,4096]{1,0:T(8,128)(2,1)S(1)}, bf16[24,4096]{1,0:T(8,128)(2,1)S(1)}, u32[]{:S(2)}, u32[]{:S(2)}) collective-permute-start(bf16[24,4096]{1,0:T(8,128)(2,1)S(1)} %get-tuple-element.9), channel_id=1, source_target_pairs={{0,8},{1,9},{2,10},{3,11},{4,12},{5,13},{6,14},{7,15},{8,0},{9,1},... | collective-permute-start | bytes 589832 | tf_op jit(solution)/shard_map/ppermute | solution.py:20
  13.9 2.3 %collective-permute-start.5 = (bf16[24,4096]{1,0:T(8,128)(2,1)S(1)}, bf16[24,4096]{1,0:T(8,128)(2,1)S(1)}, u32[]{:S(2)}, u32[]{:S(2)}) collective-permute-start(bf16[24,4096]{1,0:T(8,128)(2,1)S(1)} %get-tuple-element.10), channel_id=1, source_target_pairs={{0,6},{1,7},{2,4},{3,5},{4,2},{5,3},{6,0},{7,1},{8,14},{9,15},{10,... | collective-permute-start | bytes 589832 | tf_op jit(solution)/shard_map/ppermute | solution.py:20
  17.6 16.7 %collective-permute-start.4 = (bf16[24,4096]{1,0:T(8,128)(2,1)S(1)}, bf16[24,4096]{1,0:T(8,128)(2,1)S(1)}, u32[]{:S(2)}, u32[]{:S(2)}) collective-permute-start(bf16[24,4096]{1,0:T(8,128)(2,1)S(1)} %get-tuple-element.11), channel_id=1, source_target_pairs={{0,4},{1,5},{2,6},{3,7},{4,0},{5,1},{6,2},{7,3},{8,12},{9,13},{10,... | collective-permute-start | bytes 589832 | tf_op jit(solution)/shard_map/ppermute | solution.py:20
  34.4 1.5 collective-permute-start
  35.8 0.8 pad_maximum_fusion.4
  36.6 4.8 %collective-permute-done.11 = bf16[24,4096]{1,0:T(8,128)(2,1)S(1)} collective-permute-done((bf16[24,4096]{1,0:T(8,128)(2,1)S(1)}, bf16[24,4096]{1,0:T(8,128)(2,1)S(1)}, u32[]{:S(2)}, u32[]{:S(2)}) %collective-permute-start.11) | collective-permute-done | bytes 196640 | tf_op jit(solution)/shard_map/ppermute | solution.py:20
  41.4 1.4 collective-permute-start.18
  42.9 1.9 %collective-permute-done.10 = bf16[24,4096]{1,0:T(8,128)(2,1)S(1)} collective-permute-done((bf16[24,4096]{1,0:T(8,128)(2,1)S(1)}, bf16[24,4096]{1,0:T(8,128)(2,1)S(1)}, u32[]{:S(2)}, u32[]{:S(2)}) %collective-permute-start.10) | collective-permute-done | bytes 196640 | tf_op jit(solution)/shard_map/ppermute | solution.py:20
  44.8 0.8 pad_maximum_fusion.3
  45.5 1.5 collective-permute-start.12
  47.0 0.8 pad_maximum_fusion.2
  48.4 1.5 collective-permute-start.1
  50.1 25.9 %collective-permute-done.1 = bf16[48,4096]{1,0:T(8,128)(2,1)S(1)} collective-permute-done((bf16[48,4096]{1,0:T(8,128)(2,1)S(1)}, bf16[48,4096]{1,0:T(8,128)(2,1)S(1)}, u32[]{:S(2)}, u32[]{:S(2)}) %collective-permute-start.1) | collective-permute-done | bytes 393248 | tf_op jit(solution)/shard_map/ppermute | solution.py:20
  76.0 4.3 %fusion.22 = f32[96,896]{1,0:T(8,128)S(1)} fusion(bf16[1,4096,896]{2,1,0:T(8,128)(2,1)} %param.11, bf16[48,4096]{1,0:T(8,128)(2,1)S(1)} %collective-permute-done.1, bf16[24,4096]{1,0:T(8,128)(2,1)S(1)} %collective-permute-done, bf16[24,4096]{1,0:T(8,128)(2,1)S(1)} %get-tuple-element.5), kind=kOutput, calls=%fused_computation.22 | convolution fusion | flops 707002368 | bytes 8470528 | tf_op jit(solution)/shard_map/dot_general | solution.py:52
  80.3 9.0 %fusion.6 = f32[96,4096]{1,0:T(8,128)} fusion(bf16[1,896,4096]{2,1,0:T(8,128)(2,1)} %param.13, f32[96,896]{1,0:T(8,128)S(1)} %fusion.22, bf16[1,4096,896]{2,1,0:T(8,128)(2,1)} %param.12, bf16[48,4096]{1,0:T(8,128)(2,1)S(1)} %collective-permute-done.1, bf16[24,4096]{1,0:T(8,128)(2,1)S(1)} %collective-permute-done, bf16[24,4096]{1,0:T(8,128)(2,1)S(1)} %get-tuple-element.5), kind=kOutput, calls=%fused_computation.6 | convolution fusion | flops 1412161536 | bytes 17383424 | tf_op jit(solution)/shard_map/dot_general | solution.py:55
  89.2 1.9 %slice.243 = bf16[48,4096]{1,0:T(8,128)(2,1)} slice(f32[96,4096]{1,0:T(8,128)} %fusion.6), slice={[48:96], [0:4096]} | slice | bytes 786432 | tf_op jit(solution)/shard_map/slice | solution.py:59
  91.2 1.4 collective-permute-start.2
  92.6 1.0 constant_dynamic-update-slice_fusion.6
  93.6 4.3 %fusion.8 = f32[96,896]{1,0:T(8,128)S(1)} fusion(bf16[96,4096]{1,0:T(8,128)(2,1)S(1)} %constant_dynamic-update-slice_fusion.6, bf16[1,4096,896]{2,1,0:T(8,128)(2,1)} %param.12), kind=kOutput, calls=%fused_computation.8 | convolution fusion | flops 704643072 | bytes 8470528 | tf_op jit(solution)/shard_map/dot_general | solution.py:53
  97.9 9.0 %fusion = f32[96,4096]{1,0:T(8,128)} fusion(bf16[1,896,4096]{2,1,0:T(8,128)(2,1)} %param.13, f32[96,896]{1,0:T(8,128)S(1)} %fusion.8, bf16[96,4096]{1,0:T(8,128)(2,1)S(1)} %constant_dynamic-update-slice_fusion.6, bf16[1,4096,896]{2,1,0:T(8,128)(2,1)} %param.11), kind=kOutput, calls=%fused_computation | convolution fusion | flops 1409802240 | bytes 17383424 | tf_op jit(solution)/shard_map/dot_general | solution.py:55
  106.9 1.9 %slice.240 = bf16[48,4096]{1,0:T(8,128)(2,1)} slice(f32[96,4096]{1,0:T(8,128)} %fusion), slice={[48:96], [0:4096]} | slice | bytes 786432 | tf_op jit(solution)/shard_map/slice | solution.py:59
  109.4 1.0 constant_dynamic-update-slice_fusion.3
  110.5 4.3 %fusion.10 = f32[96,896]{1,0:T(8,128)S(1)} fusion(bf16[96,4096]{1,0:T(8,128)(2,1)S(1)} %constant_dynamic-update-slice_fusion.3, bf16[1,4096,896]{2,1,0:T(8,128)(2,1)} %param.12), kind=kOutput, calls=%fused_computation.10 | convolution fusion | flops 704643072 | bytes 8470528 | tf_op jit(solution)/shard_map/dot_general | solution.py:53
  114.8 8.0 %fusion.2 = f32[96,4096]{1,0:T(8,128)S(1)} fusion(bf16[1,896,4096]{2,1,0:T(8,128)(2,1)} %param.13, f32[96,896]{1,0:T(8,128)S(1)} %fusion.10, bf16[96,4096]{1,0:T(8,128)(2,1)S(1)} %constant_dynamic-update-slice_fusion.3, bf16[1,4096,896]{2,1,0:T(8,128)(2,1)} %param.11), kind=kOutput, calls=%fused_computation.2 | convolution fusion | flops 1409802240 | bytes 17383424 | tf_op jit(solution)/shard_map/dot_general | solution.py:55
  122.9 1.5 collective-permute-start.13
  124.4 1.0 constant_dynamic-update-slice_fusion
  125.4 4.3 %fusion.12 = f32[96,896]{1,0:T(8,128)S(1)} fusion(bf16[96,4096]{1,0:T(8,128)(2,1)S(1)} %constant_dynamic-update-slice_fusion, bf16[1,4096,896]{2,1,0:T(8,128)(2,1)} %param.12), kind=kOutput, calls=%fused_computation.12 | convolution fusion | flops 704643072 | bytes 8470528 | tf_op jit(solution)/shard_map/dot_general | solution.py:53
  129.7 9.0 %fusion.4 = f32[96,4096]{1,0:T(8,128)} fusion(bf16[1,896,4096]{2,1,0:T(8,128)(2,1)} %param.13, f32[96,896]{1,0:T(8,128)S(1)} %fusion.12, bf16[96,4096]{1,0:T(8,128)(2,1)S(1)} %constant_dynamic-update-slice_fusion, bf16[1,4096,896]{2,1,0:T(8,128)(2,1)} %param.11), kind=kOutput, calls=%fused_computation.4 | convolution fusion | flops 1409802240 | bytes 17383424 | tf_op jit(solution)/shard_map/dot_general | solution.py:55
  138.7 1.3 slice.242
  140.0 0.7 collective-permute-start.7
  140.7 1.3 fusion.38
  142.0 1.8 collective-permute-start.3
  143.8 1.1 fusion.35
  144.9 2.1 %collective-permute-start.20 = (bf16[24,4096]{1,0:T(8,128)(2,1)S(1)}, bf16[24,4096]{1,0:T(8,128)(2,1)S(1)}, u32[]{:S(2)}, u32[]{:S(2)}) collective-permute-start(bf16[24,4096]{1,0:T(8,128)(2,1)S(1)} %get-tuple-element.19), channel_id=1, source_target_pairs={{0,12},{1,13},{2,14},{3,15},{4,8},{5,9},{6,10},{7,11},{8,4},{9,5},... | collective-permute-start | bytes 589832 | tf_op jit(solution)/shard_map/ppermute | solution.py:20
  147.0 1.6 collective-permute-start.21
  148.8 3.1 %collective-permute-start.9 = (bf16[24,4096]{1,0:T(8,128)(2,1)S(1)}, bf16[24,4096]{1,0:T(8,128)(2,1)S(1)}, u32[]{:S(2)}, u32[]{:S(2)}) collective-permute-start(bf16[24,4096]{1,0:T(8,128)(2,1)S(1)} %get-tuple-element.16), channel_id=1, source_target_pairs={{0,6},{1,7},{2,4},{3,5},{4,2},{5,3},{6,0},{7,1},{8,14},{9,15},{10,... | collective-permute-start | bytes 589832 | tf_op jit(solution)/shard_map/ppermute | solution.py:20
  152.0 8.7 %collective-permute-done.8 = bf16[24,4096]{1,0:T(8,128)(2,1)S(1)} collective-permute-done((bf16[24,4096]{1,0:T(8,128)(2,1)S(1)}, bf16[24,4096]{1,0:T(8,128)(2,1)S(1)}, u32[]{:S(2)}, u32[]{:S(2)}) %collective-permute-start.8) | collective-permute-done | bytes 196640 | tf_op jit(solution)/shard_map/ppermute | solution.py:20
  160.7 2.3 %collective-permute-start.14 = (bf16[24,4096]{1,0:T(8,128)(2,1)S(1)}, bf16[24,4096]{1,0:T(8,128)(2,1)S(1)}, u32[]{:S(2)}, u32[]{:S(2)}) collective-permute-start(bf16[24,4096]{1,0:T(8,128)(2,1)S(1)} %get-tuple-element.17), channel_id=1, source_target_pairs={{0,8},{1,9},{2,10},{3,11},{4,12},{5,13},{6,14},{7,15},{8,0},{9,1},... | collective-permute-start | bytes 589832 | tf_op jit(solution)/shard_map/ppermute | solution.py:20
  163.0 1.5 collective-permute-done.9
  164.5 2.5 %collective-permute-start.15 = (bf16[24,4096]{1,0:T(8,128)(2,1)S(1)}, bf16[24,4096]{1,0:T(8,128)(2,1)S(1)}, u32[]{:S(2)}, u32[]{:S(2)}) collective-permute-start(bf16[24,4096]{1,0:T(8,128)(2,1)S(1)} %get-tuple-element.18), channel_id=1, source_target_pairs={{0,10},{1,11},{2,8},{3,9},{4,14},{5,15},{6,12},{7,13},{8,2},{9,3},... | collective-permute-start | bytes 589832 | tf_op jit(solution)/shard_map/ppermute | solution.py:20
  167.5 7.4 %collective-permute-done.14 = bf16[24,4096]{1,0:T(8,128)(2,1)S(1)} collective-permute-done((bf16[24,4096]{1,0:T(8,128)(2,1)S(1)}, bf16[24,4096]{1,0:T(8,128)(2,1)S(1)}, u32[]{:S(2)}, u32[]{:S(2)}) %collective-permute-start.14) | collective-permute-done | bytes 196640 | tf_op jit(solution)/shard_map/ppermute | solution.py:20
  174.9 3.1 %collective-permute-done.15 = bf16[24,4096]{1,0:T(8,128)(2,1)S(1)} collective-permute-done((bf16[24,4096]{1,0:T(8,128)(2,1)S(1)}, bf16[24,4096]{1,0:T(8,128)(2,1)S(1)}, u32[]{:S(2)}, u32[]{:S(2)}) %collective-permute-start.15) | collective-permute-done | bytes 196640 | tf_op jit(solution)/shard_map/ppermute | solution.py:20
  179.5 1.3 fusion.34
  (72 shorter events, 6.3 us)
Async XLA Ops:
  4.7 11.5 %copy-start.8 = (f32[64,2]{0,1:T(2,128)S(1)}, f32[64,2]{0,1:T(2,128)}, u32[]{:S(2)}) copy-start(f32[64,2]{0,1:T(2,128)} %param.9) | copy-start | bytes 1540
  4.8 12.8 %collective-permute-start.17 = (bf16[24,4096]{1,0:T(8,128)(2,1)S(1)}, bf16[24,4096]{1,0:T(8,128)(2,1)S(1)}, u32[]{:S(2)}, u32[]{:S(2)}) collective-permute-start(bf16[24,4096]{1,0:T(8,128)(2,1)S(1)} %get-tuple-element.6), channel_id=1, source_target_pairs={{0,14},{1,15},{2,12},{3,13},{4,10},{5,11},{6,8},{7,9},{8,6},{9,7},... | collective-permute-start | bytes 589832 | tf_op jit(solution)/shard_map/ppermute | solution.py:20
  10.9 23.5 %collective-permute-start.16 = (bf16[24,4096]{1,0:T(8,128)(2,1)S(1)}, bf16[24,4096]{1,0:T(8,128)(2,1)S(1)}, u32[]{:S(2)}, u32[]{:S(2)}) collective-permute-start(bf16[24,4096]{1,0:T(8,128)(2,1)S(1)} %get-tuple-element.7), channel_id=1, source_target_pairs={{0,12},{1,13},{2,14},{3,15},{4,8},{5,9},{6,10},{7,11},{8,4},{9,5},... | collective-permute-start | bytes 589832 | tf_op jit(solution)/shard_map/ppermute | solution.py:20
  11.1 30.3 %collective-permute-start.11 = (bf16[24,4096]{1,0:T(8,128)(2,1)S(1)}, bf16[24,4096]{1,0:T(8,128)(2,1)S(1)}, u32[]{:S(2)}, u32[]{:S(2)}) collective-permute-start(bf16[24,4096]{1,0:T(8,128)(2,1)S(1)} %get-tuple-element.8), channel_id=1, source_target_pairs={{0,10},{1,11},{2,8},{3,9},{4,14},{5,15},{6,12},{7,13},{8,2},{9,3},... | collective-permute-start | bytes 589832 | tf_op jit(solution)/shard_map/ppermute | solution.py:20
  11.8 32.9 %collective-permute-start.10 = (bf16[24,4096]{1,0:T(8,128)(2,1)S(1)}, bf16[24,4096]{1,0:T(8,128)(2,1)S(1)}, u32[]{:S(2)}, u32[]{:S(2)}) collective-permute-start(bf16[24,4096]{1,0:T(8,128)(2,1)S(1)} %get-tuple-element.9), channel_id=1, source_target_pairs={{0,8},{1,9},{2,10},{3,11},{4,12},{5,13},{6,14},{7,15},{8,0},{9,1},... | collective-permute-start | bytes 589832 | tf_op jit(solution)/shard_map/ppermute | solution.py:20
  13.9 33.1 %collective-permute-start.5 = (bf16[24,4096]{1,0:T(8,128)(2,1)S(1)}, bf16[24,4096]{1,0:T(8,128)(2,1)S(1)}, u32[]{:S(2)}, u32[]{:S(2)}) collective-permute-start(bf16[24,4096]{1,0:T(8,128)(2,1)S(1)} %get-tuple-element.10), channel_id=1, source_target_pairs={{0,6},{1,7},{2,4},{3,5},{4,2},{5,3},{6,0},{7,1},{8,14},{9,15},{10,... | collective-permute-start | bytes 589832 | tf_op jit(solution)/shard_map/ppermute | solution.py:20
  17.6 29.4 %collective-permute-start.4 = (bf16[24,4096]{1,0:T(8,128)(2,1)S(1)}, bf16[24,4096]{1,0:T(8,128)(2,1)S(1)}, u32[]{:S(2)}, u32[]{:S(2)}) collective-permute-start(bf16[24,4096]{1,0:T(8,128)(2,1)S(1)} %get-tuple-element.11), channel_id=1, source_target_pairs={{0,4},{1,5},{2,6},{3,7},{4,0},{5,1},{6,2},{7,3},{8,12},{9,13},{10,... | collective-permute-start | bytes 589832 | tf_op jit(solution)/shard_map/ppermute | solution.py:20
  34.4 14.0 %collective-permute-start = (bf16[24,4096]{1,0:T(8,128)(2,1)S(1)}, bf16[24,4096]{1,0:T(8,128)(2,1)S(1)}, u32[]{:S(2)}, u32[]{:S(2)}) collective-permute-start(bf16[24,4096]{1,0:T(8,128)(2,1)S(1)} %get-tuple-element.12), channel_id=1, source_target_pairs={{0,2},{1,3},{2,0},{3,1},{4,6},{5,7},{6,4},{7,5},{8,10},{9,11},{10,... | collective-permute-start | bytes 589832 | tf_op jit(solution)/shard_map/ppermute | solution.py:20
  41.4 51.2 %collective-permute-start.18 = (bf16[48,4096]{1,0:T(8,128)(2,1)}, bf16[48,4096]{1,0:T(8,128)(2,1)}, u32[]{:S(2)}, u32[]{:S(2)}) collective-permute-start(bf16[48,4096]{1,0:T(8,128)(2,1)} %pad_maximum_fusion.4), channel_id=1, source_target_pairs={{0,1},{1,0},{2,3},{3,2},{4,5},{5,4},{6,7},{7,6},{8,9},{9,8},{10,11... | collective-permute-start | bytes 1179656 | tf_op jit(solution)/shard_map/ppermute | solution.py:20
  45.5 63.9 %collective-permute-start.12 = (bf16[48,4096]{1,0:T(8,128)(2,1)}, bf16[48,4096]{1,0:T(8,128)(2,1)}, u32[]{:S(2)}, u32[]{:S(2)}) collective-permute-start(bf16[48,4096]{1,0:T(8,128)(2,1)} %pad_maximum_fusion.3), channel_id=1, source_target_pairs={{0,1},{1,0},{2,3},{3,2},{4,5},{5,4},{6,7},{7,6},{8,9},{9,8},{10,11... | collective-permute-start | bytes 1179656 | tf_op jit(solution)/shard_map/ppermute | solution.py:20
  47.0 1.4 copy-start.3
  47.8 76.5 %collective-permute-start.6 = (bf16[48,4096]{1,0:T(8,128)(2,1)}, bf16[48,4096]{1,0:T(8,128)(2,1)}, u32[]{:S(2)}, u32[]{:S(2)}) collective-permute-start(bf16[48,4096]{1,0:T(8,128)(2,1)} %pad_maximum_fusion.2), channel_id=1, source_target_pairs={{0,1},{1,0},{2,3},{3,2},{4,5},{5,4},{6,7},{7,6},{8,9},{9,8},{10,11... | collective-permute-start | bytes 1179656 | tf_op jit(solution)/shard_map/ppermute | solution.py:20
  48.4 1.6 copy-start.4
  48.4 27.5 %collective-permute-start.1 = (bf16[48,4096]{1,0:T(8,128)(2,1)S(1)}, bf16[48,4096]{1,0:T(8,128)(2,1)S(1)}, u32[]{:S(2)}, u32[]{:S(2)}) collective-permute-start(bf16[48,4096]{1,0:T(8,128)(2,1)S(1)} %pad_maximum_fusion.1), channel_id=1, source_target_pairs={{0,1},{1,0},{2,3},{3,2},{4,5},{5,4},{6,7},{7,6},{8,9},{9,8},{10,11... | collective-permute-start | bytes 1179656 | tf_op jit(solution)/shard_map/ppermute | solution.py:20
  91.2 49.5 %collective-permute-start.2 = (bf16[48,4096]{1,0:T(8,128)(2,1)}, bf16[48,4096]{1,0:T(8,128)(2,1)}, u32[]{:S(2)}, u32[]{:S(2)}) collective-permute-start(bf16[48,4096]{1,0:T(8,128)(2,1)} %slice.243), channel_id=1, source_target_pairs={{0,1},{1,0},{2,3},{3,2},{4,5},{5,4},{6,7},{7,6},{8,9},{9,8},{10,11... | collective-permute-start | bytes 1179656 | tf_op jit(solution)/shard_map/ppermute | solution.py:20
  108.9 34.9 %collective-permute-start.19 = (bf16[48,4096]{1,0:T(8,128)(2,1)}, bf16[48,4096]{1,0:T(8,128)(2,1)}, u32[]{:S(2)}, u32[]{:S(2)}) collective-permute-start(bf16[48,4096]{1,0:T(8,128)(2,1)} %slice.240), channel_id=1, source_target_pairs={{0,1},{1,0},{2,3},{3,2},{4,5},{5,4},{6,7},{7,6},{8,9},{9,8},{10,11... | collective-permute-start | bytes 1179656 | tf_op jit(solution)/shard_map/ppermute | solution.py:20
  122.9 25.9 %collective-permute-start.13 = (bf16[48,4096]{1,0:T(8,128)(2,1)S(1)}, bf16[48,4096]{1,0:T(8,128)(2,1)S(1)}, u32[]{:S(2)}, u32[]{:S(2)}) collective-permute-start(bf16[48,4096]{1,0:T(8,128)(2,1)S(1)} %slice.241), channel_id=1, source_target_pairs={{0,1},{1,0},{2,3},{3,2},{4,5},{5,4},{6,7},{7,6},{8,9},{9,8},{10,11... | collective-permute-start | bytes 1179656 | tf_op jit(solution)/shard_map/ppermute | solution.py:20
  138.7 5.1 %copy-start = (f32[96,4096]{1,0:T(8,128)S(1)}, f32[96,4096]{1,0:T(8,128)}, u32[]{:S(2)}) copy-start(f32[96,4096]{1,0:T(8,128)} %fusion) | copy-start | bytes 4718596
  140.0 8.5 %copy-start.1 = (f32[96,4096]{1,0:T(8,128)S(1)}, f32[96,4096]{1,0:T(8,128)}, u32[]{:S(2)}) copy-start(f32[96,4096]{1,0:T(8,128)} %fusion.4) | copy-start | bytes 4718596
  140.0 8.5 %collective-permute-start.7 = (bf16[48,4096]{1,0:T(8,128)(2,1)S(1)}, bf16[48,4096]{1,0:T(8,128)(2,1)S(1)}, u32[]{:S(2)}, u32[]{:S(2)}) collective-permute-start(bf16[48,4096]{1,0:T(8,128)(2,1)S(1)} %slice.242), channel_id=1, source_target_pairs={{0,1},{1,0},{2,3},{3,2},{4,5},{5,4},{6,7},{7,6},{8,9},{9,8},{10,11... | collective-permute-start | bytes 1179656 | tf_op jit(solution)/shard_map/ppermute | solution.py:20
  142.0 37.0 %collective-permute-start.3 = (bf16[24,4096]{1,0:T(8,128)(2,1)S(1)}, bf16[24,4096]{1,0:T(8,128)(2,1)S(1)}, u32[]{:S(2)}, u32[]{:S(2)}) collective-permute-start(bf16[24,4096]{1,0:T(8,128)(2,1)S(1)} %get-tuple-element.14), channel_id=1, source_target_pairs={{0,2},{1,3},{2,0},{3,1},{4,6},{5,7},{6,4},{7,5},{8,10},{9,11},{10,... | collective-permute-start | bytes 589832 | tf_op jit(solution)/shard_map/ppermute | solution.py:20
  144.9 33.6 %collective-permute-start.20 = (bf16[24,4096]{1,0:T(8,128)(2,1)S(1)}, bf16[24,4096]{1,0:T(8,128)(2,1)S(1)}, u32[]{:S(2)}, u32[]{:S(2)}) collective-permute-start(bf16[24,4096]{1,0:T(8,128)(2,1)S(1)} %get-tuple-element.19), channel_id=1, source_target_pairs={{0,12},{1,13},{2,14},{3,15},{4,8},{5,9},{6,10},{7,11},{8,4},{9,5},... | collective-permute-start | bytes 589832 | tf_op jit(solution)/shard_map/ppermute | solution.py:20
  147.0 20.1 %copy-start.6 = (pred[128,2,24]{0,2,1:T(8,128)(4,1)S(1)}, pred[128,2,24]{0,2,1:T(8,128)(4,1)}, u32[]{:S(2)}) copy-start(pred[128,2,24]{0,2,1:T(8,128)(4,1)} %get-tuple-element.24) | copy-start | bytes 18436
  147.0 20.1 %copy-start.7 = (f32[128]{0:T(128)S(1)}, f32[128]{0:T(128)}, u32[]{:S(2)}) copy-start(f32[128]{0:T(128)} %mul.93) | copy-start | bytes 1540
  147.0 31.5 %collective-permute-start.21 = (bf16[24,4096]{1,0:T(8,128)(2,1)S(1)}, bf16[24,4096]{1,0:T(8,128)(2,1)S(1)}, u32[]{:S(2)}, u32[]{:S(2)}) collective-permute-start(bf16[24,4096]{1,0:T(8,128)(2,1)S(1)} %get-tuple-element.20), channel_id=1, source_target_pairs={{0,14},{1,15},{2,12},{3,13},{4,10},{5,11},{6,8},{7,9},{8,6},{9,7},... | collective-permute-start | bytes 589832 | tf_op jit(solution)/shard_map/ppermute | solution.py:20
  148.7 12.0 %collective-permute-start.8 = (bf16[24,4096]{1,0:T(8,128)(2,1)S(1)}, bf16[24,4096]{1,0:T(8,128)(2,1)S(1)}, u32[]{:S(2)}, u32[]{:S(2)}) collective-permute-start(bf16[24,4096]{1,0:T(8,128)(2,1)S(1)} %get-tuple-element.15), channel_id=1, source_target_pairs={{0,4},{1,5},{2,6},{3,7},{4,0},{5,1},{6,2},{7,3},{8,12},{9,13},{10,... | collective-permute-start | bytes 589832 | tf_op jit(solution)/shard_map/ppermute | solution.py:20
  148.7 29.2 %copy-start.5 = (pred[128,2,24]{0,2,1:T(8,128)(4,1)S(1)}, pred[128,2,24]{0,2,1:T(8,128)(4,1)}, u32[]{:S(2)}) copy-start(pred[128,2,24]{0,2,1:T(8,128)(4,1)} %get-tuple-element.23) | copy-start | bytes 18436
  148.8 15.7 %collective-permute-start.9 = (bf16[24,4096]{1,0:T(8,128)(2,1)S(1)}, bf16[24,4096]{1,0:T(8,128)(2,1)S(1)}, u32[]{:S(2)}, u32[]{:S(2)}) collective-permute-start(bf16[24,4096]{1,0:T(8,128)(2,1)S(1)} %get-tuple-element.16), channel_id=1, source_target_pairs={{0,6},{1,7},{2,4},{3,5},{4,2},{5,3},{6,0},{7,1},{8,14},{9,15},{10,... | collective-permute-start | bytes 589832 | tf_op jit(solution)/shard_map/ppermute | solution.py:20
  160.7 14.2 %collective-permute-start.14 = (bf16[24,4096]{1,0:T(8,128)(2,1)S(1)}, bf16[24,4096]{1,0:T(8,128)(2,1)S(1)}, u32[]{:S(2)}, u32[]{:S(2)}) collective-permute-start(bf16[24,4096]{1,0:T(8,128)(2,1)S(1)} %get-tuple-element.17), channel_id=1, source_target_pairs={{0,8},{1,9},{2,10},{3,11},{4,12},{5,13},{6,14},{7,15},{8,0},{9,1},... | collective-permute-start | bytes 589832 | tf_op jit(solution)/shard_map/ppermute | solution.py:20
  164.5 13.5 %collective-permute-start.15 = (bf16[24,4096]{1,0:T(8,128)(2,1)S(1)}, bf16[24,4096]{1,0:T(8,128)(2,1)S(1)}, u32[]{:S(2)}, u32[]{:S(2)}) collective-permute-start(bf16[24,4096]{1,0:T(8,128)(2,1)S(1)} %get-tuple-element.18), channel_id=1, source_target_pairs={{0,10},{1,11},{2,8},{3,9},{4,14},{5,15},{6,12},{7,13},{8,2},{9,3},... | collective-permute-start | bytes 589832 | tf_op jit(solution)/shard_map/ppermute | solution.py:20
  178.5 1.0 copy-start.2

commit v2 on v0

v2 whole, which is shorter than its diff:
```python
import jax
import jax.numpy as jnp
from jax import lax
from jax.experimental import pallas as pl
from jax.experimental.pallas import tpu as pltpu
from jax.sharding import PartitionSpec as P


EXPERTS = 8
CAP = 24
CHUNKS = ((0, 1), (2, 3), (4,), (5,), (6,), (7,))
PREP_FLOPS = 20_000_000_000
VMEM = pl.BlockSpec(memory_space=pltpu.VMEM)


def flip(values, mask, n_devices):
    if mask == 0:
        return values
    return lax.ppermute(values, "expert", [(i, i ^ mask) for i in range(n_devices)])


def expert_kernel(blocks, *refs):
    rows_in, (w_gate, w_up, w_down), (mine, other, rows, hidden) = refs[:blocks], refs[blocks:blocks + 3], refs[blocks + 3:]
    at = 0
    for ref in rows_in:
        rows[pl.ds(at, ref.shape[0]), :] = ref[...]
        at += ref.shape[0]
    own = mine.shape[0]
    small = rows.shape[0] <= 256
    step = 128

    def first(n, carry):
        part = pl.ds(pl.multiple_of(n * step, step), step)
        both = jnp.concatenate([w_gate[0, :, part], w_up[0, :, part]], axis=1)
        acts = jnp.dot(rows[...], both, preferred_element_type=jnp.float32)
        gate_act, up_act = acts[:, :step], acts[:, step:]
        hidden[:, part] = (gate_act / (1.0 + jnp.exp(-gate_act)) * up_act).astype(jnp.bfloat16)
        return carry

    lax.fori_loop(0, w_gate.shape[2] // step, first, 0, unroll=small)
    wide = 256

    def second(n, carry):
        part = pl.ds(pl.multiple_of(n * wide, wide), wide)
        out = jnp.dot(hidden[...], w_down[0, :, part], preferred_element_type=jnp.float32)
        mine[:, part] = out[:own]
        other[:, part] = out[own:].astype(jnp.bfloat16)
        return carry

    lax.fori_loop(0, w_down.shape[2] // wide, second, 0, unroll=small)


def prepare_kernel(own_expert, ids, weights, tokens, norm_gain, *outs):
    blocks, table = outs[:EXPERTS], outs[EXPERTS]
    count = tokens.shape[0]
    wide = tokens[...].astype(jnp.float32)
    mean_square = jnp.mean(wide * wide, axis=-1, keepdims=True)
    normed = (wide * lax.rsqrt(mean_square + 1e-05) * norm_gain[...]).astype(jnp.bfloat16)
    relative = jnp.bitwise_xor(ids[...], own_expert[0])
    expert = lax.broadcasted_iota(jnp.int32, (EXPERTS, count), 0)
    first, second = relative[0:1] == expert, relative[1:2] == expert
    named = jnp.where(first | second, 1.0, 0.0)
    earlier = lax.broadcasted_iota(jnp.int32, (count, count), 0) < lax.broadcasted_iota(jnp.int32, (count, count), 1)
    rank = jnp.dot(named, jnp.where(earlier, 1.0, 0.0), preferred_element_type=jnp.float32)
    place = jnp.where(first | second, rank.astype(jnp.int32), -1)
    share = jnp.where(first, weights[0:1], jnp.where(second, weights[1:2], 0.0))
    row = lax.broadcasted_iota(jnp.int32, (CAP, count), 0)
    for r in range(EXPERTS):
        hit = place[r:r + 1] == row
        pick = jnp.where(hit, 1.0, 0.0).astype(jnp.bfloat16)
        blocks[r][...] = jnp.dot(pick, normed, preferred_element_type=jnp.float32).astype(jnp.bfloat16)
        table[r * CAP:(r + 1) * CAP, :] = jnp.where(hit, share[r:r + 1], 0.0)


def prepare(own_expert, ids, weights, tokens, norm_gain):
    count, width = tokens.shape
    *blocks, table = pl.pallas_call(
        prepare_kernel,
        out_shape=[jax.ShapeDtypeStruct((CAP, width), jnp.bfloat16)] * EXPERTS
        + [jax.ShapeDtypeStruct((EXPERTS * CAP, count), jnp.float32)],
        in_specs=[pl.BlockSpec(memory_space=pltpu.SMEM)] + [VMEM] * 4,
        out_specs=[VMEM] * (EXPERTS + 1),
        cost_estimate=pl.CostEstimate(flops=PREP_FLOPS, bytes_accessed=4 * count * width, transcendentals=count),
        compiler_params=pltpu.CompilerParams(vmem_limit_bytes=8 << 20),
    )(own_expert, ids, weights, tokens, norm_gain)
    return blocks, table


def combine_kernel(tokens, table, *refs):
    blocks, out, rows = refs[:EXPERTS], refs[EXPERTS], refs[EXPERTS + 1]
    for r in range(EXPERTS):
        rows[pl.ds(r * CAP, CAP), :] = blocks[r][...]
    share = table[...].T
    high = share.astype(jnp.bfloat16)
    low = (share - high.astype(jnp.float32)).astype(jnp.bfloat16)
    mixture = jnp.dot(high, rows[...], preferred_element_type=jnp.float32)
    mixture = mixture + jnp.dot(low, rows[...], preferred_element_type=jnp.float32)
    out[...] = (tokens[...].astype(jnp.float32) + mixture).astype(jnp.bfloat16)


def combine(tokens, table, blocks):
    count, width = tokens.shape
    return pl.pallas_call(
        combine_kernel,
        out_shape=jax.ShapeDtypeStruct((count, width), jnp.bfloat16),
        in_specs=[VMEM] * (EXPERTS + 2),
        out_specs=VMEM,
        scratch_shapes=[pltpu.VMEM((EXPERTS * CAP, width), jnp.bfloat16)],
        cost_estimate=pl.CostEstimate(flops=4 * count * EXPERTS * CAP * width, bytes_accessed=4 * count * width, transcendentals=0),
        compiler_params=pltpu.CompilerParams(vmem_limit_bytes=12 << 20),
    )(tokens, table, *blocks)


def experts(own, others, w_gate, w_up, w_down):
    count = sum(b.shape[0] for b in own)
    total = count + sum(b.shape[0] for b in others)
    width, units = w_gate.shape[1:]
    blocks = len(own) + len(others)
    return pl.pallas_call(
        lambda *refs: expert_kernel(blocks, *refs),
        out_shape=(
            jax.ShapeDtypeStruct((count, width), jnp.float32),
            jax.ShapeDtypeStruct((total - count, width), jnp.bfloat16),
        ),
        in_specs=[VMEM] * (blocks + 3),
        out_specs=(VMEM, VMEM),
        scratch_shapes=[pltpu.VMEM((total, width), jnp.bfloat16), pltpu.VMEM((total, units), jnp.bfloat16)],
        cost_estimate=pl.CostEstimate(flops=6 * max(total, 192) * width * units, bytes_accessed=6 * width * units, transcendentals=total * units),
        compiler_params=pltpu.CompilerParams(vmem_limit_bytes=(6 << 20) + total * (width + units) * 2),
    )(*own, *others, w_gate, w_up, w_down)


def body(tokens, expert_ids, route_weights, norm_gain, w_gate, w_up, w_down):
    n_devices = lax.axis_size("expert")
    shards = n_devices // EXPERTS
    own_expert = (lax.axis_index("expert") // shards).reshape(1).astype(jnp.int32)
    slots, table = prepare(own_expert, expert_ids.T, route_weights.T, tokens, norm_gain[None, :])
    mine = [flip(slots[r], r * shards, n_devices) for r in range(EXPERTS)]
    theirs = [[flip(mine[r], m, n_devices) for r in range(EXPERTS)] for m in range(1, shards)]
    back = [None] * EXPERTS
    for rs in CHUNKS:
        own = [mine[r] for r in rs]
        others = [theirs[m][r] for m in range(shards - 1) for r in rs]
        summed, part = experts(own, others, w_gate, w_up, w_down)
        rows = len(rs) * CAP
        for m in range(1, shards):
            summed = summed + flip(part[(m - 1) * rows:m * rows], m, n_devices).astype(jnp.float32)
        for i, r in enumerate(rs):
            done = summed[i * CAP:(i + 1) * CAP].astype(jnp.bfloat16)
            back[r] = flip(done, r * shards, n_devices)
    return combine(tokens, table, back)


def solution(mesh):
    in_specs = (
        P(("dp", "expert"), None),
        P(("dp", "expert"), None),
        P(("dp", "expert"), None),
        P(),
        P("expert", None, None),
        P("expert", None, None),
        P("expert", None, None),
    )
    out_specs = P(("dp", "expert"), None)
    return jax.shard_map(body, mesh=mesh, in_specs=in_specs, out_specs=out_specs, check_vma=False)
```

time: 247 us -> 120 us (0.49)
  the two profiles are of different devices: /device:TPU:14 before, /device:TPU:20 now
where the time goes in v2:
time: 120 us; the launch traced here: 119 us
  waiting for transfers between devices  48.9 us (41%)
  starting transfers between devices  38.8 us (32%)
  Pallas kernels  28 us (23%)
  local copies, waits for them, and re-layouts  3.19 us (3%)
    ppermute x28, waiting for transfers between devices, flip(): lax.ppermute(values, 'expert', [(i, i ^ mask) for i in range(n_devices)])  48.9 us
    ppermute x28, starting transfers between devices, flip(): lax.ppermute(values, 'expert', [(i, i ^ mask) for i in range(n_devices)])  38.8 us
    pallas_call x6, Pallas kernels, experts(): pl.pallas_call(lambda *refs: expert_kernel(blocks, *refs), out_shape=(jax...  25.6 us
    unnamed x16, local copies, waits for them, and re-layouts  3.13 us
  transfers between devices with their start and end apart: 28, of which 14 were waited for; matrix products, arithmetic and copies ran while one was open for 0% of the time, Pallas kernels for 21%

profile of v2, /device:TPU:20, one launch (start us, length us, event | category | flops | bytes accessed | tf_op | source)
XLA Modules:
  0.0 119.4 jit_solution(8267935386895706329)
XLA Ops:
  0.0 1.0 copy-done.3
  1.0 0.7 copy-done.5
  1.8 0.7 copy-done.6
  2.4 0.7 copy-done.7
  3.1 0.9 shard_map.73
  4.4 2.5 %collective-permute-start.16 = (bf16[24,4096]{1,0:T(8,128)(2,1)S(1)}, bf16[24,4096]{1,0:T(8,128)(2,1)S(1)}, u32[]{:S(2)}, u32[]{:S(2)}) collective-permute-start(bf16[24,4096]{1,0:T(8,128)(2,1)S(1)} %get-tuple-element.38), channel_id=1, source_target_pairs={{0,10},{1,11},{2,8},{3,9},{4,14},{5,15},{6,12},{7,13},{8,2},{9,3},... | collective-permute-start | bytes 589832 | tf_op jit(solution)/shard_map/ppermute | solution.py:19
  7.0 11.2 %collective-permute-done.12.refs_0_ = bf16[24,4096]{1,0:T(8,128)(2,1)S(1)} collective-permute-done((bf16[24,4096]{1,0:T(8,128)(2,1)S(1)}, bf16[24,4096]{1,0:T(8,128)(2,1)S(1)}, u32[]{:S(2)}, u32[]{:S(2)}) %collective-permute-start.12) | collective-permute-done | bytes 196640 | tf_op jit(solution)/shard_map/ppermute | solution.py:19
  18.1 1.5 %collective-permute-start.13 = (bf16[24,4096]{1,0:T(8,128)(2,1)S(1)}, bf16[24,4096]{1,0:T(8,128)(2,1)S(1)}, u32[]{:S(2)}, u32[]{:S(2)}) collective-permute-start(bf16[24,4096]{1,0:T(8,128)(2,1)S(1)} %collective-permute-done.12.refs_0_), channel_id=1, source_target_pairs={{0,1},{1,0},{2,3},{3,2},{4,5},{5,4},{6,7},{7,6},{8,9},{9,8},{10,11... | collective-permute-start | bytes 589832 | tf_op jit(solution)/shard_map/ppermute | solution.py:19
  19.6 1.6 %collective-permute-start.20 = (bf16[24,4096]{1,0:T(8,128)(2,1)S(1)}, bf16[24,4096]{1,0:T(8,128)(2,1)S(1)}, u32[]{:S(2)}, u32[]{:S(2)}) collective-permute-start(bf16[24,4096]{1,0:T(8,128)(2,1)S(1)} %get-tuple-element.41), channel_id=1, source_target_pairs={{0,12},{1,13},{2,14},{3,15},{4,8},{5,9},{6,10},{7,11},{8,4},{9,5},... | collective-permute-start | bytes 589832 | tf_op jit(solution)/shard_map/ppermute | solution.py:19
  21.6 5.3 %collective-permute-start.5 = (bf16[24,4096]{1,0:T(8,128)(2,1)S(1)}, bf16[24,4096]{1,0:T(8,128)(2,1)S(1)}, u32[]{:S(2)}, u32[]{:S(2)}) collective-permute-start(bf16[24,4096]{1,0:T(8,128)(2,1)S(1)} %get-tuple-element.31), channel_id=1, source_target_pairs={{0,4},{1,5},{2,6},{3,7},{4,0},{5,1},{6,2},{7,3},{8,12},{9,13},{10,... | collective-permute-start | bytes 589832 | tf_op jit(solution)/shard_map/ppermute | solution.py:19
  26.9 1.0 collective-permute-start.6
  27.8 3.1 %collective-permute-start.17 = (bf16[24,4096]{1,0:T(8,128)(2,1)S(1)}, bf16[24,4096]{1,0:T(8,128)(2,1)S(1)}, u32[]{:S(2)}, u32[]{:S(2)}) collective-permute-start(bf16[24,4096]{1,0:T(8,128)(2,1)S(1)} %collective-permute-done.16.refs_0_), channel_id=1, source_target_pairs={{0,1},{1,0},{2,3},{3,2},{4,5},{5,4},{6,7},{7,6},{8,9},{9,8},{10,11... | collective-permute-start | bytes 589832 | tf_op jit(solution)/shard_map/ppermute | solution.py:19
  30.9 4.2 %shard_map.76 = (f32[24,4096]{1,0:T(8,128)S(1)}, bf16[24,4096]{1,0:T(8,128)(2,1)S(1)}) custom-call(bf16[24,4096]{1,0:T(8,128)(2,1)S(1)} %collective-permute-done.12.refs_0_, bf16[24,4096]{1,0:T(8,128)(2,1)S(1)} %collective-permute-done.13.refs_1_, bf16[1,4096,896]{2,1,0:T(8,128)(2,1)S(1)} %copy-done, bf16[1,4096,896]{2,1,0:T(8,128)(2,1)S(1)} %copy-done.1, ...), custom_call_target="tpu_custom_call" | custom-call | flops 4227858432 | bytes 22020096 | tf_op jit(solution)/shard_map/pallas_call | solution.py:119
  35.2 1.9 %collective-permute-done.20.refs_0_ = bf16[24,4096]{1,0:T(8,128)(2,1)S(1)} collective-permute-done((bf16[24,4096]{1,0:T(8,128)(2,1)S(1)}, bf16[24,4096]{1,0:T(8,128)(2,1)S(1)}, u32[]{:S(2)}, u32[]{:S(2)}) %collective-permute-start.20) | collective-permute-done | bytes 196640 | tf_op jit(solution)/shard_map/ppermute | solution.py:19
  37.5 1.5 %collective-permute-start.21 = (bf16[24,4096]{1,0:T(8,128)(2,1)S(1)}, bf16[24,4096]{1,0:T(8,128)(2,1)S(1)}, u32[]{:S(2)}, u32[]{:S(2)}) collective-permute-start(bf16[24,4096]{1,0:T(8,128)(2,1)S(1)} %collective-permute-done.20.refs_0_), channel_id=1, source_target_pairs={{0,1},{1,0},{2,3},{3,2},{4,5},{5,4},{6,7},{7,6},{8,9},{9,8},{10,11... | collective-permute-start | bytes 589832 | tf_op jit(solution)/shard_map/ppermute | solution.py:19
  39.0 4.2 %shard_map.77 = (f32[24,4096]{1,0:T(8,128)S(1)}, bf16[24,4096]{1,0:T(8,128)(2,1)S(1)}) custom-call(bf16[24,4096]{1,0:T(8,128)(2,1)S(1)} %collective-permute-done.16.refs_0_, bf16[24,4096]{1,0:T(8,128)(2,1)S(1)} %collective-permute-done.17.refs_1_, bf16[1,4096,896]{2,1,0:T(8,128)(2,1)S(1)} %copy-done, bf16[1,4096,896]{2,1,0:T(8,128)(2,1)S(1)} %copy-done.1, ...), custom_call_target="tpu_custom_call" | custom-call | flops 4227858432 | bytes 22020096 | tf_op jit(solution)/shard_map/pallas_call | solution.py:119
  43.3 1.2 %collective-permute-done.24.refs_0_ = bf16[24,4096]{1,0:T(8,128)(2,1)S(1)} collective-permute-done((bf16[24,4096]{1,0:T(8,128)(2,1)S(1)}, bf16[24,4096]{1,0:T(8,128)(2,1)S(1)}, u32[]{:S(2)}, u32[]{:S(2)}) %collective-permute-start.24) | collective-permute-done | bytes 196640 | tf_op jit(solution)/shard_map/ppermute | solution.py:19
  44.5 0.8 collective-permute-start.1
  45.3 1.2 %collective-permute-start.25 = (bf16[24,4096]{1,0:T(8,128)(2,1)S(1)}, bf16[24,4096]{1,0:T(8,128)(2,1)S(1)}, u32[]{:S(2)}, u32[]{:S(2)}) collective-permute-start(bf16[24,4096]{1,0:T(8,128)(2,1)S(1)} %collective-permute-done.24.refs_0_), channel_id=1, source_target_pairs={{0,1},{1,0},{2,3},{3,2},{4,5},{5,4},{6,7},{7,6},{8,9},{9,8},{10,11... | collective-permute-start | bytes 589832 | tf_op jit(solution)/shard_map/ppermute | solution.py:19
  46.5 0.8 collective-permute-start.7
  47.3 1.3 %collective-permute-done.refs_1_ = bf16[24,4096]{1,0:T(8,128)(2,1)S(1)} collective-permute-done((bf16[24,4096]{1,0:T(8,128)(2,1)S(1)}, bf16[24,4096]{1,0:T(8,128)(2,1)S(1)}, u32[]{:S(2)}, u32[]{:S(2)}) %collective-permute-start) | collective-permute-done | bytes 196640 | tf_op jit(solution)/shard_map/ppermute | solution.py:19
  48.6 0.8 collective-permute-start.8
  49.4 1.2 %collective-permute-start.2 = (bf16[24,4096]{1,0:T(8,128)(2,1)S(1)}, bf16[24,4096]{1,0:T(8,128)(2,1)S(1)}, u32[]{:S(2)}, u32[]{:S(2)}) collective-permute-start(bf16[24,4096]{1,0:T(8,128)(2,1)S(1)} %collective-permute-done.refs_1_), channel_id=1, source_target_pairs={{0,1},{1,0},{2,3},{3,2},{4,5},{5,4},{6,7},{7,6},{8,9},{9,8},{10,11... | collective-permute-start | bytes 589832 | tf_op jit(solution)/shard_map/ppermute | solution.py:19
  50.6 4.2 %shard_map.78 = (f32[24,4096]{1,0:T(8,128)S(1)}, bf16[24,4096]{1,0:T(8,128)(2,1)S(1)}) custom-call(bf16[24,4096]{1,0:T(8,128)(2,1)S(1)} %collective-permute-done.20.refs_0_, bf16[24,4096]{1,0:T(8,128)(2,1)S(1)} %collective-permute-done.21.refs_1_, bf16[1,4096,896]{2,1,0:T(8,128)(2,1)S(1)} %copy-done, bf16[1,4096,896]{2,1,0:T(8,128)(2,1)S(1)} %copy-done.1, ...), custom_call_target="tpu_custom_call" | custom-call | flops 4227858432 | bytes 22020096 | tf_op jit(solution)/shard_map/pallas_call | solution.py:119
  54.9 1.6 %collective-permute-done.25.refs_1_ = bf16[24,4096]{1,0:T(8,128)(2,1)S(1)} collective-permute-done((bf16[24,4096]{1,0:T(8,128)(2,1)S(1)}, bf16[24,4096]{1,0:T(8,128)(2,1)S(1)}, u32[]{:S(2)}, u32[]{:S(2)}) %collective-permute-start.25) | collective-permute-done | bytes 196640 | tf_op jit(solution)/shard_map/ppermute | solution.py:19
  56.5 0.8 collective-permute-start.14
  57.3 4.4 %shard_map.79 = (f32[24,4096]{1,0:T(8,128)S(1)}, bf16[24,4096]{1,0:T(8,128)(2,1)S(1)}) custom-call(bf16[24,4096]{1,0:T(8,128)(2,1)S(1)} %collective-permute-done.24.refs_0_, bf16[24,4096]{1,0:T(8,128)(2,1)S(1)} %collective-permute-done.25.refs_1_, bf16[1,4096,896]{2,1,0:T(8,128)(2,1)S(1)} %copy-done, bf16[1,4096,896]{2,1,0:T(8,128)(2,1)S(1)} %copy-done.1, ...), custom_call_target="tpu_custom_call" | custom-call | flops 4227858432 | bytes 22020096 | tf_op jit(solution)/shard_map/pallas_call | solution.py:119
  61.7 1.3 %collective-permute-start.18 = (bf16[24,4096]{1,0:T(8,128)(2,1)S(1)}, bf16[24,4096]{1,0:T(8,128)(2,1)S(1)}, u32[]{:S(2)}, u32[]{:S(2)}) collective-permute-start(bf16[24,4096]{1,0:T(8,128)(2,1)S(1)} %get-tuple-element.40), channel_id=1, source_target_pairs={{0,1},{1,0},{2,3},{3,2},{4,5},{5,4},{6,7},{7,6},{8,9},{9,8},{10,11... | collective-permute-start | bytes 589832 | tf_op jit(solution)/shard_map/ppermute | solution.py:19
  63.0 1.9 %collective-permute-done.8.refs_3_ = bf16[24,4096]{1,0:T(8,128)(2,1)S(1)} collective-permute-done((bf16[24,4096]{1,0:T(8,128)(2,1)S(1)}, bf16[24,4096]{1,0:T(8,128)(2,1)S(1)}, u32[]{:S(2)}, u32[]{:S(2)}) %collective-permute-start.8) | collective-permute-done | bytes 196640 | tf_op jit(solution)/shard_map/ppermute | solution.py:19
  64.9 0.8 collective-permute-start.22
  65.7 4.2 %shard_map.75 = (f32[48,4096]{1,0:T(8,128)S(1)}, bf16[48,4096]{1,0:T(8,128)(2,1)S(1)}) custom-call(bf16[24,4096]{1,0:T(8,128)(2,1)S(1)} %collective-permute-done.5.refs_0_, bf16[24,4096]{1,0:T(8,128)(2,1)S(1)} %collective-permute-done.6.refs_1_, bf16[24,4096]{1,0:T(8,128)(2,1)S(1)} %collective-permute-done.7.refs_2_, ...), custom_call_target="tpu_custom_call" | custom-call | flops 4227858432 | bytes 22020096 | tf_op jit(solution)/shard_map/pallas_call | solution.py:119
  69.9 1.3 %collective-permute-start.26 = (bf16[24,4096]{1,0:T(8,128)(2,1)S(1)}, bf16[24,4096]{1,0:T(8,128)(2,1)S(1)}, u32[]{:S(2)}, u32[]{:S(2)}) collective-permute-start(bf16[24,4096]{1,0:T(8,128)(2,1)S(1)} %get-tuple-element.46), channel_id=1, source_target_pairs={{0,1},{1,0},{2,3},{3,2},{4,5},{5,4},{6,7},{7,6},{8,9},{9,8},{10,11... | collective-permute-start | bytes 589832 | tf_op jit(solution)/shard_map/ppermute | solution.py:19
  71.2 0.8 collective-permute-start.9
  72.0 4.2 %shard_map.74 = (f32[48,4096]{1,0:T(8,128)S(1)}, bf16[48,4096]{1,0:T(8,128)(2,1)S(1)}) custom-call(bf16[24,4096]{1,0:T(8,128)(2,1)S(1)} %get-tuple-element.27.refs_0_, bf16[24,4096]{1,0:T(8,128)(2,1)S(1)} %collective-permute-done.refs_1_, bf16[24,4096]{1,0:T(8,128)(2,1)S(1)} %collective-permute-done.1.refs_2_, ...), custom_call_target="tpu_custom_call" | custom-call | flops 4227858432 | bytes 22020096 | tf_op jit(solution)/shard_map/pallas_call | solution.py:119
  76.3 1.3 %collective-permute-start.3 = (bf16[48,4096]{1,0:T(8,128)(2,1)S(1)}, bf16[48,4096]{1,0:T(8,128)(2,1)S(1)}, u32[]{:S(2)}, u32[]{:S(2)}) collective-permute-start(bf16[48,4096]{1,0:T(8,128)(2,1)S(1)} %get-tuple-element.30), channel_id=1, source_target_pairs={{0,1},{1,0},{2,3},{3,2},{4,5},{5,4},{6,7},{7,6},{8,9},{9,8},{10,11... | collective-permute-start | bytes 1179656 | tf_op jit(solution)/shard_map/ppermute | solution.py:19
  78.2 3.5 %collective-permute-done.22 = bf16[24,4096]{1,0:T(8,128)(2,1)S(1)} collective-permute-done((bf16[24,4096]{1,0:T(8,128)(2,1)S(1)}, bf16[24,4096]{1,0:T(8,128)(2,1)S(1)}, u32[]{:S(2)}, u32[]{:S(2)}) %collective-permute-start.22) | collective-permute-done | bytes 196640 | tf_op jit(solution)/shard_map/ppermute | solution.py:19
  81.8 1.2 collective-permute-start.19
  83.0 3.0 %collective-permute-done.26 = bf16[24,4096]{1,0:T(8,128)(2,1)S(1)} collective-permute-done((bf16[24,4096]{1,0:T(8,128)(2,1)S(1)}, bf16[24,4096]{1,0:T(8,128)(2,1)S(1)}, u32[]{:S(2)}, u32[]{:S(2)}) %collective-permute-start.26) | collective-permute-done | bytes 196640 | tf_op jit(solution)/shard_map/ppermute | solution.py:19
  86.0 2.8 %collective-permute-start.23 = (bf16[24,4096]{1,0:T(8,128)(2,1)S(1)}, bf16[24,4096]{1,0:T(8,128)(2,1)S(1)}, u32[]{:S(2)}, u32[]{:S(2)}) collective-permute-start(bf16[24,4096]{1,0:T(8,128)(2,1)S(1)} %add_convert_fusion.3), channel_id=1, source_target_pairs={{0,12},{1,13},{2,14},{3,15},{4,8},{5,9},{6,10},{7,11},{8,4},{9,5},... | collective-permute-start | bytes 589832 | tf_op jit(solution)/shard_map/ppermute | solution.py:19
  88.8 5.6 %collective-permute-done.9 = bf16[48,4096]{1,0:T(8,128)(2,1)S(1)} collective-permute-done((bf16[48,4096]{1,0:T(8,128)(2,1)S(1)}, bf16[48,4096]{1,0:T(8,128)(2,1)S(1)}, u32[]{:S(2)}, u32[]{:S(2)}) %collective-permute-start.9) | collective-permute-done | bytes 393248 | tf_op jit(solution)/shard_map/ppermute | solution.py:19
  94.4 1.9 %collective-permute-start.27 = (bf16[24,4096]{1,0:T(8,128)(2,1)S(1)}, bf16[24,4096]{1,0:T(8,128)(2,1)S(1)}, u32[]{:S(2)}, u32[]{:S(2)}) collective-permute-start(bf16[24,4096]{1,0:T(8,128)(2,1)S(1)} %add_convert_fusion.2), channel_id=1, source_target_pairs={{0,14},{1,15},{2,12},{3,13},{4,10},{5,11},{6,8},{7,9},{8,6},{9,7},... | collective-permute-start | bytes 589832 | tf_op jit(solution)/shard_map/ppermute | solution.py:19
  96.4 5.2 %collective-permute-done.3 = bf16[48,4096]{1,0:T(8,128)(2,1)S(1)} collective-permute-done((bf16[48,4096]{1,0:T(8,128)(2,1)S(1)}, bf16[48,4096]{1,0:T(8,128)(2,1)S(1)}, u32[]{:S(2)}, u32[]{:S(2)}) %collective-permute-start.3) | collective-permute-done | bytes 393248 | tf_op jit(solution)/shard_map/ppermute | solution.py:19
  101.7 3.1 %collective-permute-start.11 = (bf16[24,4096]{1,0:T(8,128)(2,1)S(1)}, bf16[24,4096]{1,0:T(8,128)(2,1)S(1)}, u32[]{:S(2)}, u32[]{:S(2)}) collective-permute-start(bf16[24,4096]{1,0:T(8,128)(2,1)S(1)} %get-tuple-element.47), channel_id=1, source_target_pairs={{0,6},{1,7},{2,4},{3,5},{4,2},{5,3},{6,0},{7,1},{8,14},{9,15},{10,... | collective-permute-start | bytes 589832 | tf_op jit(solution)/shard_map/ppermute | solution.py:19
  105.3 2.7 %collective-permute-done.23.refs_6_ = bf16[24,4096]{1,0:T(8,128)(2,1)S(1)} collective-permute-done((bf16[24,4096]{1,0:T(8,128)(2,1)S(1)}, bf16[24,4096]{1,0:T(8,128)(2,1)S(1)}, u32[]{:S(2)}, u32[]{:S(2)}) %collective-permute-start.23) | collective-permute-done | bytes 196640 | tf_op jit(solution)/shard_map/ppermute | solution.py:19
  108.0 4.9 %collective-permute-done.27.refs_7_ = bf16[24,4096]{1,0:T(8,128)(2,1)S(1)} collective-permute-done((bf16[24,4096]{1,0:T(8,128)(2,1)S(1)}, bf16[24,4096]{1,0:T(8,128)(2,1)S(1)}, u32[]{:S(2)}, u32[]{:S(2)}) %collective-permute-start.27) | collective-permute-done | bytes 196640 | tf_op jit(solution)/shard_map/ppermute | solution.py:19
  112.9 1.1 collective-permute-done.11.refs_3_
  114.0 3.9 %collective-permute-done.4.refs_1_ = bf16[24,4096]{1,0:T(8,128)(2,1)S(1)} collective-permute-done((bf16[24,4096]{1,0:T(8,128)(2,1)S(1)}, bf16[24,4096]{1,0:T(8,128)(2,1)S(1)}, u32[]{:S(2)}, u32[]{:S(2)}) %collective-permute-start.4) | collective-permute-done | bytes 196640 | tf_op jit(solution)/shard_map/ppermute | solution.py:19
  117.9 1.6 %shard_map.80 = bf16[64,4096]{1,0:T(8,128)(2,1)} custom-call(bf16[64,4096]{1,0:T(8,128)(2,1)S(1)} %copy-done.4, f32[192,64]{1,0:T(8,128)S(1)} %get-tuple-element.26.table, bf16[24,4096]{1,0:T(8,128)(2,1)S(1)} %get-tuple-element.50.refs_0_, bf16[24,4096]{1,0:T(8,128)(2,1)S(1)} %collective-permute-done.4.refs_1_, ...), custom_call_target="tpu_custom_call" | custom-call | flops 201326592 | bytes 1048576 | tf_op jit(solution)/shard_map/pallas_call | solution.py:103
  (40 shorter events, 2.8 us)
Async XLA Ops:
  0.0 1.0 copy-start.3
  1.0 0.7 copy-start.5
  1.8 0.7 copy-start.6
  2.4 0.7 copy-start.7
  3.1 27.8 %copy-start = (bf16[1,4096,896]{2,1,0:T(8,128)(2,1)S(1)}, bf16[1,4096,896]{2,1,0:T(8,128)(2,1)}, u32[]{:S(2)}) copy-start(bf16[1,4096,896]{2,1,0:T(8,128)(2,1)} %refs_2_.7) | copy-start | bytes 22020100
  3.1 27.8 %copy-start.1 = (bf16[1,4096,896]{2,1,0:T(8,128)(2,1)S(1)}, bf16[1,4096,896]{2,1,0:T(8,128)(2,1)}, u32[]{:S(2)}) copy-start(bf16[1,4096,896]{2,1,0:T(8,128)(2,1)} %refs_3_.7) | copy-start | bytes 22020100
  3.1 27.8 %copy-start.2 = (bf16[1,896,4096]{2,1,0:T(8,128)(2,1)S(1)}, bf16[1,896,4096]{2,1,0:T(8,128)(2,1)}, u32[]{:S(2)}) copy-start(bf16[1,896,4096]{2,1,0:T(8,128)(2,1)} %refs_4_.11) | copy-start | bytes 22020100
  4.0 14.1 %collective-permute-start.12 = (bf16[24,4096]{1,0:T(8,128)(2,1)S(1)}, bf16[24,4096]{1,0:T(8,128)(2,1)S(1)}, u32[]{:S(2)}, u32[]{:S(2)}) collective-permute-start(bf16[24,4096]{1,0:T(8,128)(2,1)S(1)} %get-tuple-element.35), channel_id=1, source_target_pairs={{0,8},{1,9},{2,10},{3,11},{4,12},{5,13},{6,14},{7,15},{8,0},{9,1},... | collective-permute-start | bytes 589832 | tf_op jit(solution)/shard_map/ppermute | solution.py:19
  4.4 22.4 %collective-permute-start.16 = (bf16[24,4096]{1,0:T(8,128)(2,1)S(1)}, bf16[24,4096]{1,0:T(8,128)(2,1)S(1)}, u32[]{:S(2)}, u32[]{:S(2)}) collective-permute-start(bf16[24,4096]{1,0:T(8,128)(2,1)S(1)} %get-tuple-element.38), channel_id=1, source_target_pairs={{0,10},{1,11},{2,8},{3,9},{4,14},{5,15},{6,12},{7,13},{8,2},{9,3},... | collective-permute-start | bytes 589832 | tf_op jit(solution)/shard_map/ppermute | solution.py:19
  18.1 9.7 %collective-permute-start.13 = (bf16[24,4096]{1,0:T(8,128)(2,1)S(1)}, bf16[24,4096]{1,0:T(8,128)(2,1)S(1)}, u32[]{:S(2)}, u32[]{:S(2)}) collective-permute-start(bf16[24,4096]{1,0:T(8,128)(2,1)S(1)} %collective-permute-done.12.refs_0_), channel_id=1, source_target_pairs={{0,1},{1,0},{2,3},{3,2},{4,5},{5,4},{6,7},{7,6},{8,9},{9,8},{10,11... | collective-permute-start | bytes 589832 | tf_op jit(solution)/shard_map/ppermute | solution.py:19
  19.6 17.4 %collective-permute-start.20 = (bf16[24,4096]{1,0:T(8,128)(2,1)S(1)}, bf16[24,4096]{1,0:T(8,128)(2,1)S(1)}, u32[]{:S(2)}, u32[]{:S(2)}) collective-permute-start(bf16[24,4096]{1,0:T(8,128)(2,1)S(1)} %get-tuple-element.41), channel_id=1, source_target_pairs={{0,12},{1,13},{2,14},{3,15},{4,8},{5,9},{6,10},{7,11},{8,4},{9,5},... | collective-permute-start | bytes 589832 | tf_op jit(solution)/shard_map/ppermute | solution.py:19
  21.2 23.3 %collective-permute-start.24 = (bf16[24,4096]{1,0:T(8,128)(2,1)S(1)}, bf16[24,4096]{1,0:T(8,128)(2,1)S(1)}, u32[]{:S(2)}, u32[]{:S(2)}) collective-permute-start(bf16[24,4096]{1,0:T(8,128)(2,1)S(1)} %get-tuple-element.44), channel_id=1, source_target_pairs={{0,14},{1,15},{2,12},{3,13},{4,10},{5,11},{6,8},{7,9},{8,6},{9,7},... | collective-permute-start | bytes 589832 | tf_op jit(solution)/shard_map/ppermute | solution.py:19
  21.6 23.7 %collective-permute-start.5 = (bf16[24,4096]{1,0:T(8,128)(2,1)S(1)}, bf16[24,4096]{1,0:T(8,128)(2,1)S(1)}, u32[]{:S(2)}, u32[]{:S(2)}) collective-permute-start(bf16[24,4096]{1,0:T(8,128)(2,1)S(1)} %get-tuple-element.31), channel_id=1, source_target_pairs={{0,4},{1,5},{2,6},{3,7},{4,0},{5,1},{6,2},{7,3},{8,12},{9,13},{10,... | collective-permute-start | bytes 589832 | tf_op jit(solution)/shard_map/ppermute | solution.py:19
  26.9 19.6 %collective-permute-start.6 = (bf16[24,4096]{1,0:T(8,128)(2,1)S(1)}, bf16[24,4096]{1,0:T(8,128)(2,1)S(1)}, u32[]{:S(2)}, u32[]{:S(2)}) collective-permute-start(bf16[24,4096]{1,0:T(8,128)(2,1)S(1)} %get-tuple-element.32), channel_id=1, source_target_pairs={{0,6},{1,7},{2,4},{3,5},{4,2},{5,3},{6,0},{7,1},{8,14},{9,15},{10,... | collective-permute-start | bytes 589832 | tf_op jit(solution)/shard_map/ppermute | solution.py:19
  27.8 9.7 %collective-permute-start.17 = (bf16[24,4096]{1,0:T(8,128)(2,1)S(1)}, bf16[24,4096]{1,0:T(8,128)(2,1)S(1)}, u32[]{:S(2)}, u32[]{:S(2)}) collective-permute-start(bf16[24,4096]{1,0:T(8,128)(2,1)S(1)} %collective-permute-done.16.refs_0_), channel_id=1, source_target_pairs={{0,1},{1,0},{2,3},{3,2},{4,5},{5,4},{6,7},{7,6},{8,9},{9,8},{10,11... | collective-permute-start | bytes 589832 | tf_op jit(solution)/shard_map/ppermute | solution.py:19
  37.0 11.6 %collective-permute-start = (bf16[24,4096]{1,0:T(8,128)(2,1)S(1)}, bf16[24,4096]{1,0:T(8,128)(2,1)S(1)}, u32[]{:S(2)}, u32[]{:S(2)}) collective-permute-start(bf16[24,4096]{1,0:T(8,128)(2,1)S(1)} %get-tuple-element.28), channel_id=1, source_target_pairs={{0,2},{1,3},{2,0},{3,1},{4,6},{5,7},{6,4},{7,5},{8,10},{9,11},{10,... | collective-permute-start | bytes 589832 | tf_op jit(solution)/shard_map/ppermute | solution.py:19
  37.5 11.9 %collective-permute-start.21 = (bf16[24,4096]{1,0:T(8,128)(2,1)S(1)}, bf16[24,4096]{1,0:T(8,128)(2,1)S(1)}, u32[]{:S(2)}, u32[]{:S(2)}) collective-permute-start(bf16[24,4096]{1,0:T(8,128)(2,1)S(1)} %collective-permute-done.20.refs_0_), channel_id=1, source_target_pairs={{0,1},{1,0},{2,3},{3,2},{4,5},{5,4},{6,7},{7,6},{8,9},{9,8},{10,11... | collective-permute-start | bytes 589832 | tf_op jit(solution)/shard_map/ppermute | solution.py:19
  44.5 25.5 %collective-permute-start.1 = (bf16[24,4096]{1,0:T(8,128)(2,1)S(1)}, bf16[24,4096]{1,0:T(8,128)(2,1)S(1)}, u32[]{:S(2)}, u32[]{:S(2)}) collective-permute-start(bf16[24,4096]{1,0:T(8,128)(2,1)S(1)} %get-tuple-element.27.refs_0_), channel_id=1, source_target_pairs={{0,1},{1,0},{2,3},{3,2},{4,5},{5,4},{6,7},{7,6},{8,9},{9,8},{10,11... | collective-permute-start | bytes 589832 | tf_op jit(solution)/shard_map/ppermute | solution.py:19
  45.3 11.2 %collective-permute-start.25 = (bf16[24,4096]{1,0:T(8,128)(2,1)S(1)}, bf16[24,4096]{1,0:T(8,128)(2,1)S(1)}, u32[]{:S(2)}, u32[]{:S(2)}) collective-permute-start(bf16[24,4096]{1,0:T(8,128)(2,1)S(1)} %collective-permute-done.24.refs_0_), channel_id=1, source_target_pairs={{0,1},{1,0},{2,3},{3,2},{4,5},{5,4},{6,7},{7,6},{8,9},{9,8},{10,11... | collective-permute-start | bytes 589832 | tf_op jit(solution)/shard_map/ppermute | solution.py:19
  46.5 15.2 %collective-permute-start.7 = (bf16[24,4096]{1,0:T(8,128)(2,1)S(1)}, bf16[24,4096]{1,0:T(8,128)(2,1)S(1)}, u32[]{:S(2)}, u32[]{:S(2)}) collective-permute-start(bf16[24,4096]{1,0:T(8,128)(2,1)S(1)} %collective-permute-done.5.refs_0_), channel_id=1, source_target_pairs={{0,1},{1,0},{2,3},{3,2},{4,5},{5,4},{6,7},{7,6},{8,9},{9,8},{10,11... | collective-permute-start | bytes 589832 | tf_op jit(solution)/shard_map/ppermute | solution.py:19
  48.6 16.3 %collective-permute-start.8 = (bf16[24,4096]{1,0:T(8,128)(2,1)S(1)}, bf16[24,4096]{1,0:T(8,128)(2,1)S(1)}, u32[]{:S(2)}, u32[]{:S(2)}) collective-permute-start(bf16[24,4096]{1,0:T(8,128)(2,1)S(1)} %collective-permute-done.6.refs_1_), channel_id=1, source_target_pairs={{0,1},{1,0},{2,3},{3,2},{4,5},{5,4},{6,7},{7,6},{8,9},{9,8},{10,11... | collective-permute-start | bytes 589832 | tf_op jit(solution)/shard_map/ppermute | solution.py:19
  49.4 21.8 %collective-permute-start.2 = (bf16[24,4096]{1,0:T(8,128)(2,1)S(1)}, bf16[24,4096]{1,0:T(8,128)(2,1)S(1)}, u32[]{:S(2)}, u32[]{:S(2)}) collective-permute-start(bf16[24,4096]{1,0:T(8,128)(2,1)S(1)} %collective-permute-done.refs_1_), channel_id=1, source_target_pairs={{0,1},{1,0},{2,3},{3,2},{4,5},{5,4},{6,7},{7,6},{8,9},{9,8},{10,11... | collective-permute-start | bytes 589832 | tf_op jit(solution)/shard_map/ppermute | solution.py:19
  56.5 19.8 %collective-permute-start.14 = (bf16[24,4096]{1,0:T(8,128)(2,1)S(1)}, bf16[24,4096]{1,0:T(8,128)(2,1)S(1)}, u32[]{:S(2)}, u32[]{:S(2)}) collective-permute-start(bf16[24,4096]{1,0:T(8,128)(2,1)S(1)} %get-tuple-element.37), channel_id=1, source_target_pairs={{0,1},{1,0},{2,3},{3,2},{4,5},{5,4},{6,7},{7,6},{8,9},{9,8},{10,11... | collective-permute-start | bytes 589832 | tf_op jit(solution)/shard_map/ppermute | solution.py:19
  61.7 15.9 %collective-permute-start.18 = (bf16[24,4096]{1,0:T(8,128)(2,1)S(1)}, bf16[24,4096]{1,0:T(8,128)(2,1)S(1)}, u32[]{:S(2)}, u32[]{:S(2)}) collective-permute-start(bf16[24,4096]{1,0:T(8,128)(2,1)S(1)} %get-tuple-element.40), channel_id=1, source_target_pairs={{0,1},{1,0},{2,3},{3,2},{4,5},{5,4},{6,7},{7,6},{8,9},{9,8},{10,11... | collective-permute-start | bytes 589832 | tf_op jit(solution)/shard_map/ppermute | solution.py:19
  64.9 16.9 %collective-permute-start.22 = (bf16[24,4096]{1,0:T(8,128)(2,1)S(1)}, bf16[24,4096]{1,0:T(8,128)(2,1)S(1)}, u32[]{:S(2)}, u32[]{:S(2)}) collective-permute-start(bf16[24,4096]{1,0:T(8,128)(2,1)S(1)} %get-tuple-element.43), channel_id=1, source_target_pairs={{0,1},{1,0},{2,3},{3,2},{4,5},{5,4},{6,7},{7,6},{8,9},{9,8},{10,11... | collective-permute-start | bytes 589832 | tf_op jit(solution)/shard_map/ppermute | solution.py:19
  69.9 16.0 %collective-permute-start.26 = (bf16[24,4096]{1,0:T(8,128)(2,1)S(1)}, bf16[24,4096]{1,0:T(8,128)(2,1)S(1)}, u32[]{:S(2)}, u32[]{:S(2)}) collective-permute-start(bf16[24,4096]{1,0:T(8,128)(2,1)S(1)} %get-tuple-element.46), channel_id=1, source_target_pairs={{0,1},{1,0},{2,3},{3,2},{4,5},{5,4},{6,7},{7,6},{8,9},{9,8},{10,11... | collective-permute-start | bytes 589832 | tf_op jit(solution)/shard_map/ppermute | solution.py:19
  71.2 23.2 %collective-permute-start.9 = (bf16[48,4096]{1,0:T(8,128)(2,1)S(1)}, bf16[48,4096]{1,0:T(8,128)(2,1)S(1)}, u32[]{:S(2)}, u32[]{:S(2)}) collective-permute-start(bf16[48,4096]{1,0:T(8,128)(2,1)S(1)} %get-tuple-element.34), channel_id=1, source_target_pairs={{0,1},{1,0},{2,3},{3,2},{4,5},{5,4},{6,7},{7,6},{8,9},{9,8},{10,11... | collective-permute-start | bytes 1179656 | tf_op jit(solution)/shard_map/ppermute | solution.py:19
  76.3 41.6 %copy-start.4 = (bf16[64,4096]{1,0:T(8,128)(2,1)S(1)}, bf16[64,4096]{1,0:T(8,128)(2,1)}, u32[]{:S(2)}) copy-start(bf16[64,4096]{1,0:T(8,128)(2,1)} %tokens.3) | copy-start | bytes 1572868
  76.3 25.3 %collective-permute-start.3 = (bf16[48,4096]{1,0:T(8,128)(2,1)S(1)}, bf16[48,4096]{1,0:T(8,128)(2,1)S(1)}, u32[]{:S(2)}, u32[]{:S(2)}) collective-permute-start(bf16[48,4096]{1,0:T(8,128)(2,1)S(1)} %get-tuple-element.30), channel_id=1, source_target_pairs={{0,1},{1,0},{2,3},{3,2},{4,5},{5,4},{6,7},{7,6},{8,9},{9,8},{10,11... | collective-permute-start | bytes 1179656 | tf_op jit(solution)/shard_map/ppermute | solution.py:19
  77.6 24.1 %collective-permute-start.15 = (bf16[24,4096]{1,0:T(8,128)(2,1)S(1)}, bf16[24,4096]{1,0:T(8,128)(2,1)S(1)}, u32[]{:S(2)}, u32[]{:S(2)}) collective-permute-start(bf16[24,4096]{1,0:T(8,128)(2,1)S(1)} %add_convert_fusion.5), channel_id=1, source_target_pairs={{0,8},{1,9},{2,10},{3,11},{4,12},{5,13},{6,14},{7,15},{8,0},{9,1},... | collective-permute-start | bytes 589832 | tf_op jit(solution)/shard_map/ppermute | solution.py:19
  81.8 23.0 %collective-permute-start.19 = (bf16[24,4096]{1,0:T(8,128)(2,1)S(1)}, bf16[24,4096]{1,0:T(8,128)(2,1)S(1)}, u32[]{:S(2)}, u32[]{:S(2)}) collective-permute-start(bf16[24,4096]{1,0:T(8,128)(2,1)S(1)} %add_convert_fusion.4), channel_id=1, source_target_pairs={{0,10},{1,11},{2,8},{3,9},{4,14},{5,15},{6,12},{7,13},{8,2},{9,3},... | collective-permute-start | bytes 589832 | tf_op jit(solution)/shard_map/ppermute | solution.py:19
  86.0 22.0 %collective-permute-start.23 = (bf16[24,4096]{1,0:T(8,128)(2,1)S(1)}, bf16[24,4096]{1,0:T(8,128)(2,1)S(1)}, u32[]{:S(2)}, u32[]{:S(2)}) collective-permute-start(bf16[24,4096]{1,0:T(8,128)(2,1)S(1)} %add_convert_fusion.3), channel_id=1, source_target_pairs={{0,12},{1,13},{2,14},{3,15},{4,8},{5,9},{6,10},{7,11},{8,4},{9,5},... | collective-permute-start | bytes 589832 | tf_op jit(solution)/shard_map/ppermute | solution.py:19
  94.4 18.5 %collective-permute-start.27 = (bf16[24,4096]{1,0:T(8,128)(2,1)S(1)}, bf16[24,4096]{1,0:T(8,128)(2,1)S(1)}, u32[]{:S(2)}, u32[]{:S(2)}) collective-permute-start(bf16[24,4096]{1,0:T(8,128)(2,1)S(1)} %add_convert_fusion.2), channel_id=1, source_target_pairs={{0,14},{1,15},{2,12},{3,13},{4,10},{5,11},{6,8},{7,9},{8,6},{9,7},... | collective-permute-start | bytes 589832 | tf_op jit(solution)/shard_map/ppermute | solution.py:19
  101.6 11.3 %collective-permute-start.10 = (bf16[24,4096]{1,0:T(8,128)(2,1)S(1)}, bf16[24,4096]{1,0:T(8,128)(2,1)S(1)}, u32[]{:S(2)}, u32[]{:S(2)}) collective-permute-start(bf16[24,4096]{1,0:T(8,128)(2,1)S(1)} %get-tuple-element.48), channel_id=1, source_target_pairs={{0,4},{1,5},{2,6},{3,7},{4,0},{5,1},{6,2},{7,3},{8,12},{9,13},{10,... | collective-permute-start | bytes 589832 | tf_op jit(solution)/shard_map/ppermute | solution.py:19
  101.7 12.3 %collective-permute-start.11 = (bf16[24,4096]{1,0:T(8,128)(2,1)S(1)}, bf16[24,4096]{1,0:T(8,128)(2,1)S(1)}, u32[]{:S(2)}, u32[]{:S(2)}) collective-permute-start(bf16[24,4096]{1,0:T(8,128)(2,1)S(1)} %get-tuple-element.47), channel_id=1, source_target_pairs={{0,6},{1,7},{2,4},{3,5},{4,2},{5,3},{6,0},{7,1},{8,14},{9,15},{10,... | collective-permute-start | bytes 589832 | tf_op jit(solution)/shard_map/ppermute | solution.py:19
  104.8 13.1 %collective-permute-start.4 = (bf16[24,4096]{1,0:T(8,128)(2,1)S(1)}, bf16[24,4096]{1,0:T(8,128)(2,1)S(1)}, u32[]{:S(2)}, u32[]{:S(2)}) collective-permute-start(bf16[24,4096]{1,0:T(8,128)(2,1)S(1)} %get-tuple-element.49), channel_id=1, source_target_pairs={{0,2},{1,3},{2,0},{3,1},{4,6},{5,7},{6,4},{7,5},{8,10},{9,11},{10,... | collective-permute-start | bytes 589832 | tf_op jit(solution)/shard_map/ppermute | solution.py:19

commit v3 on v2

--- a/solution.py
+++ b/solution.py
@@ -8,7 +8,7 @@
 
 EXPERTS = 8
 CAP = 24
-CHUNKS = ((0, 1), (2, 3), (4,), (5,), (6,), (7,))
+CHUNKS = ((0, 1), (2, 3), (4, 5), (6, 7))
 PREP_FLOPS = 20_000_000_000
 VMEM = pl.BlockSpec(memory_space=pltpu.VMEM)
 
@@ -50,8 +50,15 @@
     lax.fori_loop(0, w_down.shape[2] // wide, second, 0, unroll=small)
 
 
-def prepare_kernel(own_expert, ids, weights, tokens, norm_gain, *outs):
-    blocks, table = outs[:EXPERTS], outs[EXPERTS]
+def prepare_kernel(own_expert, *refs):
+    given, blocks, table = refs[:4], refs[4:4 + EXPERTS], refs[4 + EXPERTS]
+    held, sems = refs[5 + EXPERTS:9 + EXPERTS], refs[9 + EXPERTS]
+    ids, weights, tokens, norm_gain = held
+    copies = [pltpu.make_async_copy(a, b, sems.at[i]) for i, (a, b) in enumerate(zip(given, held))]
+    for copy in copies:
+        copy.start()
+    for copy in copies:
+        copy.wait()
     count = tokens.shape[0]
     wide = tokens[...].astype(jnp.float32)
     mean_square = jnp.mean(wide * wide, axis=-1, keepdims=True)
@@ -74,15 +81,17 @@
 
 def prepare(own_expert, ids, weights, tokens, norm_gain):
     count, width = tokens.shape
+    given = [pltpu.with_memory_space_constraint(a, pltpu.HBM) for a in (ids, weights, tokens, norm_gain)]
     *blocks, table = pl.pallas_call(
         prepare_kernel,
         out_shape=[jax.ShapeDtypeStruct((CAP, width), jnp.bfloat16)] * EXPERTS
         + [jax.ShapeDtypeStruct((EXPERTS * CAP, count), jnp.float32)],
-        in_specs=[pl.BlockSpec(memory_space=pltpu.SMEM)] + [VMEM] * 4,
+        in_specs=[pl.BlockSpec(memory_space=pltpu.SMEM)] + [pl.BlockSpec(memory_space=pltpu.HBM)] * 4,
         out_specs=[VMEM] * (EXPERTS + 1),
+        scratch_shapes=[pltpu.VMEM(a.shape, a.dtype) for a in given] + [pltpu.SemaphoreType.DMA((4,))],
         cost_estimate=pl.CostEstimate(flops=PREP_FLOPS, bytes_accessed=4 * count * width, transcendentals=count),
         compiler_params=pltpu.CompilerParams(vmem_limit_bytes=8 << 20),
-    )(own_expert, ids, weights, tokens, norm_gain)
+    )(own_expert, *given)
     return blocks, table
 
 

time: 120 us -> 120 us (level)
  the two profiles are of different devices: /device:TPU:20 before, /device:TPU:0 now
where the time goes in v3:
time: 120 us
  starting transfers between devices  50.3 us (42%)
  waiting for transfers between devices  48.4 us (40%)
  Pallas kernels  20.7 us (17%)
    ppermute x26, starting transfers between devices, flip(): lax.ppermute(values, 'expert', [(i, i ^ mask) for i in range(n_devices)])  50.3 us
    ppermute x26, waiting for transfers between devices, flip(): lax.ppermute(values, 'expert', [(i, i ^ mask) for i in range(n_devices)])  48.4 us
    pallas_call x4, Pallas kernels, experts(): pl.pallas_call(lambda *refs: expert_kernel(blocks, *refs), out_shape=(jax...  17 us
  transfers between devices with their start and end apart: 26, of which 17 were waited for; matrix products, arithmetic and copies ran while one was open for 0% of the time, Pallas kernels for 14%

profile of v3, /device:TPU:0, one launch (start us, length us, event | category | flops | bytes accessed | tf_op | source)
XLA Modules:
  0.0 120.1 jit_solution(16729004823749126702)
XLA Ops:
  0.0 2.2 %shard_map.73 = (bf16[24,4096]{1,0:T(8,128)(2,1)S(1)}, bf16[24,4096]{1,0:T(8,128)(2,1)S(1)}, bf16[24,4096]{1,0:T(8,128)(2,1)S(1)}, bf16[24,4096]{1,0:T(8,128)(2,...) custom-call(s32[1]{0:T(128)} %bitcast.own_expert, ...), custom_call_target="tpu_custom_call" | custom-call | flops 20000000000 | bytes 1048576 | tf_op jit(solution)/shard_map/pallas_call | solution.py:85
  2.2 5.2 %collective-permute-start.19 = (bf16[24,4096]{1,0:T(8,128)(2,1)S(1)}, bf16[24,4096]{1,0:T(8,128)(2,1)S(1)}, u32[]{:S(2)}, u32[]{:S(2)}) collective-permute-start(bf16[24,4096]{1,0:T(8,128)(2,1)S(1)} %get-tuple-element.35), channel_id=1, source_target_pairs={{0,12},{1,13},{2,14},{3,15},{4,8},{5,9},{6,10},{7,11},{8,4},{9,5},... | collective-permute-start | bytes 589832 | tf_op jit(solution)/shard_map/ppermute | solution.py:19
  7.3 1.2 collective-permute-start.20
  8.5 0.8 collective-permute-start.12
  9.3 1.9 %collective-permute-start.13 = (bf16[24,4096]{1,0:T(8,128)(2,1)S(1)}, bf16[24,4096]{1,0:T(8,128)(2,1)S(1)}, u32[]{:S(2)}, u32[]{:S(2)}) collective-permute-start(bf16[24,4096]{1,0:T(8,128)(2,1)S(1)} %get-tuple-element.32), channel_id=1, source_target_pairs={{0,10},{1,11},{2,8},{3,9},{4,14},{5,15},{6,12},{7,13},{8,2},{9,3},... | collective-permute-start | bytes 589832 | tf_op jit(solution)/shard_map/ppermute | solution.py:19
  11.2 1.4 %collective-permute-done.19.refs_0_ = bf16[24,4096]{1,0:T(8,128)(2,1)S(1)} collective-permute-done((bf16[24,4096]{1,0:T(8,128)(2,1)S(1)}, bf16[24,4096]{1,0:T(8,128)(2,1)S(1)}, u32[]{:S(2)}, u32[]{:S(2)}) %collective-permute-start.19) | collective-permute-done | bytes 196640 | tf_op jit(solution)/shard_map/ppermute | solution.py:19
  12.6 1.5 %collective-permute-start.21 = (bf16[24,4096]{1,0:T(8,128)(2,1)S(1)}, bf16[24,4096]{1,0:T(8,128)(2,1)S(1)}, u32[]{:S(2)}, u32[]{:S(2)}) collective-permute-start(bf16[24,4096]{1,0:T(8,128)(2,1)S(1)} %collective-permute-done.19.refs_0_), channel_id=1, source_target_pairs={{0,1},{1,0},{2,3},{3,2},{4,5},{5,4},{6,7},{7,6},{8,9},{9,8},{10,11... | collective-permute-start | bytes 589832 | tf_op jit(solution)/shard_map/ppermute | solution.py:19
  14.1 4.4 %collective-permute-done.20.refs_1_ = bf16[24,4096]{1,0:T(8,128)(2,1)S(1)} collective-permute-done((bf16[24,4096]{1,0:T(8,128)(2,1)S(1)}, bf16[24,4096]{1,0:T(8,128)(2,1)S(1)}, u32[]{:S(2)}, u32[]{:S(2)}) %collective-permute-start.20) | collective-permute-done | bytes 196640 | tf_op jit(solution)/shard_map/ppermute | solution.py:19
  18.5 1.5 %collective-permute-start.22 = (bf16[24,4096]{1,0:T(8,128)(2,1)S(1)}, bf16[24,4096]{1,0:T(8,128)(2,1)S(1)}, u32[]{:S(2)}, u32[]{:S(2)}) collective-permute-start(bf16[24,4096]{1,0:T(8,128)(2,1)S(1)} %collective-permute-done.20.refs_1_), channel_id=1, source_target_pairs={{0,1},{1,0},{2,3},{3,2},{4,5},{5,4},{6,7},{7,6},{8,9},{9,8},{10,11... | collective-permute-start | bytes 589832 | tf_op jit(solution)/shard_map/ppermute | solution.py:19
  20.0 16.4 %collective-permute-start.5 = (bf16[24,4096]{1,0:T(8,128)(2,1)S(1)}, bf16[24,4096]{1,0:T(8,128)(2,1)S(1)}, u32[]{:S(2)}, u32[]{:S(2)}) collective-permute-start(bf16[24,4096]{1,0:T(8,128)(2,1)S(1)} %get-tuple-element.27), channel_id=1, source_target_pairs={{0,4},{1,5},{2,6},{3,7},{4,0},{5,1},{6,2},{7,3},{8,12},{9,13},{10,... | collective-permute-start | bytes 589832 | tf_op jit(solution)/shard_map/ppermute | solution.py:19
  36.4 1.3 %collective-permute-done.12.refs_0_ = bf16[24,4096]{1,0:T(8,128)(2,1)S(1)} collective-permute-done((bf16[24,4096]{1,0:T(8,128)(2,1)S(1)}, bf16[24,4096]{1,0:T(8,128)(2,1)S(1)}, u32[]{:S(2)}, u32[]{:S(2)}) %collective-permute-start.12) | collective-permute-done | bytes 196640 | tf_op jit(solution)/shard_map/ppermute | solution.py:19
  37.7 0.7 collective-permute-start.6
  38.5 3.5 %collective-permute-done.13.refs_1_ = bf16[24,4096]{1,0:T(8,128)(2,1)S(1)} collective-permute-done((bf16[24,4096]{1,0:T(8,128)(2,1)S(1)}, bf16[24,4096]{1,0:T(8,128)(2,1)S(1)}, u32[]{:S(2)}, u32[]{:S(2)}) %collective-permute-start.13) | collective-permute-done | bytes 196640 | tf_op jit(solution)/shard_map/ppermute | solution.py:19
  41.9 0.5 collective-permute-start
  42.4 1.5 %collective-permute-start.14 = (bf16[24,4096]{1,0:T(8,128)(2,1)S(1)}, bf16[24,4096]{1,0:T(8,128)(2,1)S(1)}, u32[]{:S(2)}, u32[]{:S(2)}) collective-permute-start(bf16[24,4096]{1,0:T(8,128)(2,1)S(1)} %collective-permute-done.12.refs_0_), channel_id=1, source_target_pairs={{0,1},{1,0},{2,3},{3,2},{4,5},{5,4},{6,7},{7,6},{8,9},{9,8},{10,11... | collective-permute-start | bytes 589832 | tf_op jit(solution)/shard_map/ppermute | solution.py:19
  43.9 0.5 collective-permute-start.15
  44.5 4.2 %shard_map.77 = (f32[48,4096]{1,0:T(8,128)S(1)}, bf16[48,4096]{1,0:T(8,128)(2,1)S(1)}) custom-call(bf16[24,4096]{1,0:T(8,128)(2,1)S(1)} %collective-permute-done.19.refs_0_, bf16[24,4096]{1,0:T(8,128)(2,1)S(1)} %collective-permute-done.20.refs_1_, bf16[24,4096]{1,0:T(8,128)(2,1)S(1)} %collective-permute-done.21.refs_2_, ...), custom_call_target="tpu_custom_call" | custom-call | flops 4227858432 | bytes 22020096 | tf_op jit(solution)/shard_map/pallas_call | solution.py:128
  48.7 1.6 %collective-permute-start.1 = (bf16[24,4096]{1,0:T(8,128)(2,1)S(1)}, bf16[24,4096]{1,0:T(8,128)(2,1)S(1)}, u32[]{:S(2)}, u32[]{:S(2)}) collective-permute-start(bf16[24,4096]{1,0:T(8,128)(2,1)S(1)} %get-tuple-element.23.refs_0_), channel_id=1, source_target_pairs={{0,1},{1,0},{2,3},{3,2},{4,5},{5,4},{6,7},{7,6},{8,9},{9,8},{10,11... | collective-permute-start | bytes 589832 | tf_op jit(solution)/shard_map/ppermute | solution.py:19
  50.3 0.1 collective-permute-done.6.refs_1_
  50.4 1.4 %collective-permute-start.7 = (bf16[24,4096]{1,0:T(8,128)(2,1)S(1)}, bf16[24,4096]{1,0:T(8,128)(2,1)S(1)}, u32[]{:S(2)}, u32[]{:S(2)}) collective-permute-start(bf16[24,4096]{1,0:T(8,128)(2,1)S(1)} %collective-permute-done.5.refs_0_), channel_id=1, source_target_pairs={{0,1},{1,0},{2,3},{3,2},{4,5},{5,4},{6,7},{7,6},{8,9},{9,8},{10,11... | collective-permute-start | bytes 589832 | tf_op jit(solution)/shard_map/ppermute | solution.py:19
  51.8 0.3 collective-permute-done.refs_1_
  52.1 1.5 %collective-permute-start.8 = (bf16[24,4096]{1,0:T(8,128)(2,1)S(1)}, bf16[24,4096]{1,0:T(8,128)(2,1)S(1)}, u32[]{:S(2)}, u32[]{:S(2)}) collective-permute-start(bf16[24,4096]{1,0:T(8,128)(2,1)S(1)} %collective-permute-done.6.refs_1_), channel_id=1, source_target_pairs={{0,1},{1,0},{2,3},{3,2},{4,5},{5,4},{6,7},{7,6},{8,9},{9,8},{10,11... | collective-permute-start | bytes 589832 | tf_op jit(solution)/shard_map/ppermute | solution.py:19
  53.6 0.5 collective-permute-start.2
  54.1 0.3 collective-permute-done.15.refs_3_
  54.4 1.5 %collective-permute-start.23 = (bf16[48,4096]{1,0:T(8,128)(2,1)S(1)}, bf16[48,4096]{1,0:T(8,128)(2,1)S(1)}, u32[]{:S(2)}, u32[]{:S(2)}) collective-permute-start(bf16[48,4096]{1,0:T(8,128)(2,1)S(1)} %get-tuple-element.38), channel_id=1, source_target_pairs={{0,1},{1,0},{2,3},{3,2},{4,5},{5,4},{6,7},{7,6},{8,9},{9,8},{10,11... | collective-permute-start | bytes 1179656 | tf_op jit(solution)/shard_map/ppermute | solution.py:19
  55.9 4.2 %shard_map.76 = (f32[48,4096]{1,0:T(8,128)S(1)}, bf16[48,4096]{1,0:T(8,128)(2,1)S(1)}) custom-call(bf16[24,4096]{1,0:T(8,128)(2,1)S(1)} %collective-permute-done.12.refs_0_, bf16[24,4096]{1,0:T(8,128)(2,1)S(1)} %collective-permute-done.13.refs_1_, bf16[24,4096]{1,0:T(8,128)(2,1)S(1)} %collective-permute-done.14.refs_2_, ...), custom_call_target="tpu_custom_call" | custom-call | flops 4227858432 | bytes 22020096 | tf_op jit(solution)/shard_map/pallas_call | solution.py:128
  60.1 2.7 %collective-permute-done.7.refs_2_ = bf16[24,4096]{1,0:T(8,128)(2,1)S(1)} collective-permute-done((bf16[24,4096]{1,0:T(8,128)(2,1)S(1)}, bf16[24,4096]{1,0:T(8,128)(2,1)S(1)}, u32[]{:S(2)}, u32[]{:S(2)}) %collective-permute-start.7) | collective-permute-done | bytes 196640 | tf_op jit(solution)/shard_map/ppermute | solution.py:19
  62.9 1.5 %collective-permute-start.16 = (bf16[48,4096]{1,0:T(8,128)(2,1)S(1)}, bf16[48,4096]{1,0:T(8,128)(2,1)S(1)}, u32[]{:S(2)}, u32[]{:S(2)}) collective-permute-start(bf16[48,4096]{1,0:T(8,128)(2,1)S(1)} %get-tuple-element.34), channel_id=1, source_target_pairs={{0,1},{1,0},{2,3},{3,2},{4,5},{5,4},{6,7},{7,6},{8,9},{9,8},{10,11... | collective-permute-start | bytes 1179656 | tf_op jit(solution)/shard_map/ppermute | solution.py:19
  64.3 2.7 %collective-permute-done.8.refs_3_ = bf16[24,4096]{1,0:T(8,128)(2,1)S(1)} collective-permute-done((bf16[24,4096]{1,0:T(8,128)(2,1)S(1)}, bf16[24,4096]{1,0:T(8,128)(2,1)S(1)}, u32[]{:S(2)}, u32[]{:S(2)}) %collective-permute-start.8) | collective-permute-done | bytes 196640 | tf_op jit(solution)/shard_map/ppermute | solution.py:19
  67.1 4.4 %shard_map.75 = (f32[48,4096]{1,0:T(8,128)S(1)}, bf16[48,4096]{1,0:T(8,128)(2,1)S(1)}) custom-call(bf16[24,4096]{1,0:T(8,128)(2,1)S(1)} %collective-permute-done.5.refs_0_, bf16[24,4096]{1,0:T(8,128)(2,1)S(1)} %collective-permute-done.6.refs_1_, bf16[24,4096]{1,0:T(8,128)(2,1)S(1)} %collective-permute-done.7.refs_2_, ...), custom_call_target="tpu_custom_call" | custom-call | flops 4227858432 | bytes 22020096 | tf_op jit(solution)/shard_map/pallas_call | solution.py:128
  71.5 1.5 %collective-permute-start.9 = (bf16[48,4096]{1,0:T(8,128)(2,1)S(1)}, bf16[48,4096]{1,0:T(8,128)(2,1)S(1)}, u32[]{:S(2)}, u32[]{:S(2)}) collective-permute-start(bf16[48,4096]{1,0:T(8,128)(2,1)S(1)} %get-tuple-element.30), channel_id=1, source_target_pairs={{0,1},{1,0},{2,3},{3,2},{4,5},{5,4},{6,7},{7,6},{8,9},{9,8},{10,11... | collective-permute-start | bytes 1179656 | tf_op jit(solution)/shard_map/ppermute | solution.py:19
  73.0 4.2 %shard_map.74 = (f32[48,4096]{1,0:T(8,128)S(1)}, bf16[48,4096]{1,0:T(8,128)(2,1)S(1)}) custom-call(bf16[24,4096]{1,0:T(8,128)(2,1)S(1)} %get-tuple-element.23.refs_0_, bf16[24,4096]{1,0:T(8,128)(2,1)S(1)} %collective-permute-done.refs_1_, bf16[24,4096]{1,0:T(8,128)(2,1)S(1)} %collective-permute-done.1.refs_2_, ...), custom_call_target="tpu_custom_call" | custom-call | flops 4227858432 | bytes 22020096 | tf_op jit(solution)/shard_map/pallas_call | solution.py:128
  77.3 0.6 collective-permute-start.3
  77.9 1.8 %collective-permute-done.23 = bf16[48,4096]{1,0:T(8,128)(2,1)S(1)} collective-permute-done((bf16[48,4096]{1,0:T(8,128)(2,1)S(1)}, bf16[48,4096]{1,0:T(8,128)(2,1)S(1)}, u32[]{:S(2)}, u32[]{:S(2)}) %collective-permute-start.23) | collective-permute-done | bytes 393248 | tf_op jit(solution)/shard_map/ppermute | solution.py:19
  79.8 2.5 %collective-permute-start.24 = (bf16[24,4096]{1,0:T(8,128)(2,1)S(1)}, bf16[24,4096]{1,0:T(8,128)(2,1)S(1)}, u32[]{:S(2)}, u32[]{:S(2)}) collective-permute-start(bf16[24,4096]{1,0:T(8,128)(2,1)S(1)} %get-tuple-element.40), channel_id=1, source_target_pairs={{0,12},{1,13},{2,14},{3,15},{4,8},{5,9},{6,10},{7,11},{8,4},{9,5},... | collective-permute-start | bytes 589832 | tf_op jit(solution)/shard_map/ppermute | solution.py:19
  82.4 2.3 %collective-permute-start.25 = (bf16[24,4096]{1,0:T(8,128)(2,1)S(1)}, bf16[24,4096]{1,0:T(8,128)(2,1)S(1)}, u32[]{:S(2)}, u32[]{:S(2)}) collective-permute-start(bf16[24,4096]{1,0:T(8,128)(2,1)S(1)} %get-tuple-element.39), channel_id=1, source_target_pairs={{0,14},{1,15},{2,12},{3,13},{4,10},{5,11},{6,8},{7,9},{8,6},{9,7},... | collective-permute-start | bytes 589832 | tf_op jit(solution)/shard_map/ppermute | solution.py:19
  84.7 3.5 %collective-permute-done.16 = bf16[48,4096]{1,0:T(8,128)(2,1)S(1)} collective-permute-done((bf16[48,4096]{1,0:T(8,128)(2,1)S(1)}, bf16[48,4096]{1,0:T(8,128)(2,1)S(1)}, u32[]{:S(2)}, u32[]{:S(2)}) %collective-permute-start.16) | collective-permute-done | bytes 393248 | tf_op jit(solution)/shard_map/ppermute | solution.py:19
  88.1 0.1 add_convert_fusion.1
  88.3 8.2 %collective-permute-done.9 = bf16[48,4096]{1,0:T(8,128)(2,1)S(1)} collective-permute-done((bf16[48,4096]{1,0:T(8,128)(2,1)S(1)}, bf16[48,4096]{1,0:T(8,128)(2,1)S(1)}, u32[]{:S(2)}, u32[]{:S(2)}) %collective-permute-start.9) | collective-permute-done | bytes 393248 | tf_op jit(solution)/shard_map/ppermute | solution.py:19
  96.7 6.2 %collective-permute-done.3 = bf16[48,4096]{1,0:T(8,128)(2,1)S(1)} collective-permute-done((bf16[48,4096]{1,0:T(8,128)(2,1)S(1)}, bf16[48,4096]{1,0:T(8,128)(2,1)S(1)}, u32[]{:S(2)}, u32[]{:S(2)}) %collective-permute-start.3) | collective-permute-done | bytes 393248 | tf_op jit(solution)/shard_map/ppermute | solution.py:19
  102.8 0.1 add_convert_fusion.3
  103.0 3.0 %collective-permute-start.11 = (bf16[24,4096]{1,0:T(8,128)(2,1)S(1)}, bf16[24,4096]{1,0:T(8,128)(2,1)S(1)}, u32[]{:S(2)}, u32[]{:S(2)}) collective-permute-start(bf16[24,4096]{1,0:T(8,128)(2,1)S(1)} %get-tuple-element.43), channel_id=1, source_target_pairs={{0,6},{1,7},{2,4},{3,5},{4,2},{5,3},{6,0},{7,1},{8,14},{9,15},{10,... | collective-permute-start | bytes 589832 | tf_op jit(solution)/shard_map/ppermute | solution.py:19
  106.0 0.5 collective-permute-start.4
  106.5 2.3 %collective-permute-done.17.refs_4_ = bf16[24,4096]{1,0:T(8,128)(2,1)S(1)} collective-permute-done((bf16[24,4096]{1,0:T(8,128)(2,1)S(1)}, bf16[24,4096]{1,0:T(8,128)(2,1)S(1)}, u32[]{:S(2)}, u32[]{:S(2)}) %collective-permute-start.17) | collective-permute-done | bytes 196640 | tf_op jit(solution)/shard_map/ppermute | solution.py:19
  108.8 2.0 %collective-permute-done.18.refs_5_ = bf16[24,4096]{1,0:T(8,128)(2,1)S(1)} collective-permute-done((bf16[24,4096]{1,0:T(8,128)(2,1)S(1)}, bf16[24,4096]{1,0:T(8,128)(2,1)S(1)}, u32[]{:S(2)}, u32[]{:S(2)}) %collective-permute-start.18) | collective-permute-done | bytes 196640 | tf_op jit(solution)/shard_map/ppermute | solution.py:19
  110.9 4.3 %collective-permute-done.10.refs_2_ = bf16[24,4096]{1,0:T(8,128)(2,1)S(1)} collective-permute-done((bf16[24,4096]{1,0:T(8,128)(2,1)S(1)}, bf16[24,4096]{1,0:T(8,128)(2,1)S(1)}, u32[]{:S(2)}, u32[]{:S(2)}) %collective-permute-start.10) | collective-permute-done | bytes 196640 | tf_op jit(solution)/shard_map/ppermute | solution.py:19
  115.1 3.3 %collective-permute-done.11.refs_3_ = bf16[24,4096]{1,0:T(8,128)(2,1)S(1)} collective-permute-done((bf16[24,4096]{1,0:T(8,128)(2,1)S(1)}, bf16[24,4096]{1,0:T(8,128)(2,1)S(1)}, u32[]{:S(2)}, u32[]{:S(2)}) %collective-permute-start.11) | collective-permute-done | bytes 196640 | tf_op jit(solution)/shard_map/ppermute | solution.py:19
  118.5 1.6 %shard_map.78 = bf16[64,4096]{1,0:T(8,128)(2,1)} custom-call(bf16[64,4096]{1,0:T(8,128)(2,1)S(1)} %copy-done.3, f32[192,64]{1,0:T(8,128)S(1)} %get-tuple-element.22.table, bf16[24,4096]{1,0:T(8,128)(2,1)S(1)} %get-tuple-element.46.refs_0_, bf16[24,4096]{1,0:T(8,128)(2,1)S(1)} %collective-permute-done.4.refs_1_, ...), custom_call_target="tpu_custom_call" | custom-call | flops 201326592 | bytes 1048576 | tf_op jit(solution)/shard_map/pallas_call | solution.py:112
  (26 shorter events, 0.4 us)
Async XLA Ops:
  0.0 44.5 %copy-start = (bf16[1,4096,896]{2,1,0:T(8,128)(2,1)S(1)}, bf16[1,4096,896]{2,1,0:T(8,128)(2,1)}, u32[]{:S(2)}) copy-start(bf16[1,4096,896]{2,1,0:T(8,128)(2,1)} %refs_4_.7) | copy-start | bytes 22020100
  0.0 44.5 %copy-start.1 = (bf16[1,4096,896]{2,1,0:T(8,128)(2,1)S(1)}, bf16[1,4096,896]{2,1,0:T(8,128)(2,1)}, u32[]{:S(2)}) copy-start(bf16[1,4096,896]{2,1,0:T(8,128)(2,1)} %refs_5_.7) | copy-start | bytes 22020100
  0.0 44.5 %copy-start.2 = (bf16[1,896,4096]{2,1,0:T(8,128)(2,1)S(1)}, bf16[1,896,4096]{2,1,0:T(8,128)(2,1)}, u32[]{:S(2)}) copy-start(bf16[1,896,4096]{2,1,0:T(8,128)(2,1)} %refs_6_.7) | copy-start | bytes 22020100
  2.2 10.4 %collective-permute-start.19 = (bf16[24,4096]{1,0:T(8,128)(2,1)S(1)}, bf16[24,4096]{1,0:T(8,128)(2,1)S(1)}, u32[]{:S(2)}, u32[]{:S(2)}) collective-permute-start(bf16[24,4096]{1,0:T(8,128)(2,1)S(1)} %get-tuple-element.35), channel_id=1, source_target_pairs={{0,12},{1,13},{2,14},{3,15},{4,8},{5,9},{6,10},{7,11},{8,4},{9,5},... | collective-permute-start | bytes 589832 | tf_op jit(solution)/shard_map/ppermute | solution.py:19
  7.3 11.2 %collective-permute-start.20 = (bf16[24,4096]{1,0:T(8,128)(2,1)S(1)}, bf16[24,4096]{1,0:T(8,128)(2,1)S(1)}, u32[]{:S(2)}, u32[]{:S(2)}) collective-permute-start(bf16[24,4096]{1,0:T(8,128)(2,1)S(1)} %get-tuple-element.36), channel_id=1, source_target_pairs={{0,14},{1,15},{2,12},{3,13},{4,10},{5,11},{6,8},{7,9},{8,6},{9,7},... | collective-permute-start | bytes 589832 | tf_op jit(solution)/shard_map/ppermute | solution.py:19
  8.5 29.2 %collective-permute-start.12 = (bf16[24,4096]{1,0:T(8,128)(2,1)S(1)}, bf16[24,4096]{1,0:T(8,128)(2,1)S(1)}, u32[]{:S(2)}, u32[]{:S(2)}) collective-permute-start(bf16[24,4096]{1,0:T(8,128)(2,1)S(1)} %get-tuple-element.31), channel_id=1, source_target_pairs={{0,8},{1,9},{2,10},{3,11},{4,12},{5,13},{6,14},{7,15},{8,0},{9,1},... | collective-permute-start | bytes 589832 | tf_op jit(solution)/shard_map/ppermute | solution.py:19
  9.3 32.6 %collective-permute-start.13 = (bf16[24,4096]{1,0:T(8,128)(2,1)S(1)}, bf16[24,4096]{1,0:T(8,128)(2,1)S(1)}, u32[]{:S(2)}, u32[]{:S(2)}) collective-permute-start(bf16[24,4096]{1,0:T(8,128)(2,1)S(1)} %get-tuple-element.32), channel_id=1, source_target_pairs={{0,10},{1,11},{2,8},{3,9},{4,14},{5,15},{6,12},{7,13},{8,2},{9,3},... | collective-permute-start | bytes 589832 | tf_op jit(solution)/shard_map/ppermute | solution.py:19
  12.6 29.8 %collective-permute-start.21 = (bf16[24,4096]{1,0:T(8,128)(2,1)S(1)}, bf16[24,4096]{1,0:T(8,128)(2,1)S(1)}, u32[]{:S(2)}, u32[]{:S(2)}) collective-permute-start(bf16[24,4096]{1,0:T(8,128)(2,1)S(1)} %collective-permute-done.19.refs_0_), channel_id=1, source_target_pairs={{0,1},{1,0},{2,3},{3,2},{4,5},{5,4},{6,7},{7,6},{8,9},{9,8},{10,11... | collective-permute-start | bytes 589832 | tf_op jit(solution)/shard_map/ppermute | solution.py:19
  18.5 25.4 %collective-permute-start.22 = (bf16[24,4096]{1,0:T(8,128)(2,1)S(1)}, bf16[24,4096]{1,0:T(8,128)(2,1)S(1)}, u32[]{:S(2)}, u32[]{:S(2)}) collective-permute-start(bf16[24,4096]{1,0:T(8,128)(2,1)S(1)} %collective-permute-done.20.refs_1_), channel_id=1, source_target_pairs={{0,1},{1,0},{2,3},{3,2},{4,5},{5,4},{6,7},{7,6},{8,9},{9,8},{10,11... | collective-permute-start | bytes 589832 | tf_op jit(solution)/shard_map/ppermute | solution.py:19
  20.0 28.7 %collective-permute-start.5 = (bf16[24,4096]{1,0:T(8,128)(2,1)S(1)}, bf16[24,4096]{1,0:T(8,128)(2,1)S(1)}, u32[]{:S(2)}, u32[]{:S(2)}) collective-permute-start(bf16[24,4096]{1,0:T(8,128)(2,1)S(1)} %get-tuple-element.27), channel_id=1, source_target_pairs={{0,4},{1,5},{2,6},{3,7},{4,0},{5,1},{6,2},{7,3},{8,12},{9,13},{10,... | collective-permute-start | bytes 589832 | tf_op jit(solution)/shard_map/ppermute | solution.py:19
  37.7 12.7 %collective-permute-start.6 = (bf16[24,4096]{1,0:T(8,128)(2,1)S(1)}, bf16[24,4096]{1,0:T(8,128)(2,1)S(1)}, u32[]{:S(2)}, u32[]{:S(2)}) collective-permute-start(bf16[24,4096]{1,0:T(8,128)(2,1)S(1)} %get-tuple-element.28), channel_id=1, source_target_pairs={{0,6},{1,7},{2,4},{3,5},{4,2},{5,3},{6,0},{7,1},{8,14},{9,15},{10,... | collective-permute-start | bytes 589832 | tf_op jit(solution)/shard_map/ppermute | solution.py:19
  41.9 10.1 %collective-permute-start = (bf16[24,4096]{1,0:T(8,128)(2,1)S(1)}, bf16[24,4096]{1,0:T(8,128)(2,1)S(1)}, u32[]{:S(2)}, u32[]{:S(2)}) collective-permute-start(bf16[24,4096]{1,0:T(8,128)(2,1)S(1)} %get-tuple-element.24), channel_id=1, source_target_pairs={{0,2},{1,3},{2,0},{3,1},{4,6},{5,7},{6,4},{7,5},{8,10},{9,11},{10,... | collective-permute-start | bytes 589832 | tf_op jit(solution)/shard_map/ppermute | solution.py:19
  42.4 11.1 %collective-permute-start.14 = (bf16[24,4096]{1,0:T(8,128)(2,1)S(1)}, bf16[24,4096]{1,0:T(8,128)(2,1)S(1)}, u32[]{:S(2)}, u32[]{:S(2)}) collective-permute-start(bf16[24,4096]{1,0:T(8,128)(2,1)S(1)} %collective-permute-done.12.refs_0_), channel_id=1, source_target_pairs={{0,1},{1,0},{2,3},{3,2},{4,5},{5,4},{6,7},{7,6},{8,9},{9,8},{10,11... | collective-permute-start | bytes 589832 | tf_op jit(solution)/shard_map/ppermute | solution.py:19
  43.9 10.5 %collective-permute-start.15 = (bf16[24,4096]{1,0:T(8,128)(2,1)S(1)}, bf16[24,4096]{1,0:T(8,128)(2,1)S(1)}, u32[]{:S(2)}, u32[]{:S(2)}) collective-permute-start(bf16[24,4096]{1,0:T(8,128)(2,1)S(1)} %collective-permute-done.13.refs_1_), channel_id=1, source_target_pairs={{0,1},{1,0},{2,3},{3,2},{4,5},{5,4},{6,7},{7,6},{8,9},{9,8},{10,11... | collective-permute-start | bytes 589832 | tf_op jit(solution)/shard_map/ppermute | solution.py:19
  48.7 24.3 %collective-permute-start.1 = (bf16[24,4096]{1,0:T(8,128)(2,1)S(1)}, bf16[24,4096]{1,0:T(8,128)(2,1)S(1)}, u32[]{:S(2)}, u32[]{:S(2)}) collective-permute-start(bf16[24,4096]{1,0:T(8,128)(2,1)S(1)} %get-tuple-element.23.refs_0_), channel_id=1, source_target_pairs={{0,1},{1,0},{2,3},{3,2},{4,5},{5,4},{6,7},{7,6},{8,9},{9,8},{10,11... | collective-permute-start | bytes 589832 | tf_op jit(solution)/shard_map/ppermute | solution.py:19
  50.4 12.5 %collective-permute-start.7 = (bf16[24,4096]{1,0:T(8,128)(2,1)S(1)}, bf16[24,4096]{1,0:T(8,128)(2,1)S(1)}, u32[]{:S(2)}, u32[]{:S(2)}) collective-permute-start(bf16[24,4096]{1,0:T(8,128)(2,1)S(1)} %collective-permute-done.5.refs_0_), channel_id=1, source_target_pairs={{0,1},{1,0},{2,3},{3,2},{4,5},{5,4},{6,7},{7,6},{8,9},{9,8},{10,11... | collective-permute-start | bytes 589832 | tf_op jit(solution)/shard_map/ppermute | solution.py:19
  52.1 15.0 %collective-permute-start.8 = (bf16[24,4096]{1,0:T(8,128)(2,1)S(1)}, bf16[24,4096]{1,0:T(8,128)(2,1)S(1)}, u32[]{:S(2)}, u32[]{:S(2)}) collective-permute-start(bf16[24,4096]{1,0:T(8,128)(2,1)S(1)} %collective-permute-done.6.refs_1_), channel_id=1, source_target_pairs={{0,1},{1,0},{2,3},{3,2},{4,5},{5,4},{6,7},{7,6},{8,9},{9,8},{10,11... | collective-permute-start | bytes 589832 | tf_op jit(solution)/shard_map/ppermute | solution.py:19
  53.6 19.5 %collective-permute-start.2 = (bf16[24,4096]{1,0:T(8,128)(2,1)S(1)}, bf16[24,4096]{1,0:T(8,128)(2,1)S(1)}, u32[]{:S(2)}, u32[]{:S(2)}) collective-permute-start(bf16[24,4096]{1,0:T(8,128)(2,1)S(1)} %collective-permute-done.refs_1_), channel_id=1, source_target_pairs={{0,1},{1,0},{2,3},{3,2},{4,5},{5,4},{6,7},{7,6},{8,9},{9,8},{10,11... | collective-permute-start | bytes 589832 | tf_op jit(solution)/shard_map/ppermute | solution.py:19
  54.4 25.3 %collective-permute-start.23 = (bf16[48,4096]{1,0:T(8,128)(2,1)S(1)}, bf16[48,4096]{1,0:T(8,128)(2,1)S(1)}, u32[]{:S(2)}, u32[]{:S(2)}) collective-permute-start(bf16[48,4096]{1,0:T(8,128)(2,1)S(1)} %get-tuple-element.38), channel_id=1, source_target_pairs={{0,1},{1,0},{2,3},{3,2},{4,5},{5,4},{6,7},{7,6},{8,9},{9,8},{10,11... | collective-permute-start | bytes 1179656 | tf_op jit(solution)/shard_map/ppermute | solution.py:19
  62.9 25.3 %collective-permute-start.16 = (bf16[48,4096]{1,0:T(8,128)(2,1)S(1)}, bf16[48,4096]{1,0:T(8,128)(2,1)S(1)}, u32[]{:S(2)}, u32[]{:S(2)}) collective-permute-start(bf16[48,4096]{1,0:T(8,128)(2,1)S(1)} %get-tuple-element.34), channel_id=1, source_target_pairs={{0,1},{1,0},{2,3},{3,2},{4,5},{5,4},{6,7},{7,6},{8,9},{9,8},{10,11... | collective-permute-start | bytes 1179656 | tf_op jit(solution)/shard_map/ppermute | solution.py:19
  71.5 25.1 %collective-permute-start.9 = (bf16[48,4096]{1,0:T(8,128)(2,1)S(1)}, bf16[48,4096]{1,0:T(8,128)(2,1)S(1)}, u32[]{:S(2)}, u32[]{:S(2)}) collective-permute-start(bf16[48,4096]{1,0:T(8,128)(2,1)S(1)} %get-tuple-element.30), channel_id=1, source_target_pairs={{0,1},{1,0},{2,3},{3,2},{4,5},{5,4},{6,7},{7,6},{8,9},{9,8},{10,11... | collective-permute-start | bytes 1179656 | tf_op jit(solution)/shard_map/ppermute | solution.py:19
  77.2 41.3 %copy-start.3 = (bf16[64,4096]{1,0:T(8,128)(2,1)S(1)}, bf16[64,4096]{1,0:T(8,128)(2,1)}, u32[]{:S(2)}) copy-start(bf16[64,4096]{1,0:T(8,128)(2,1)} %tokens.1) | copy-start | bytes 1572868
  77.3 25.6 %collective-permute-start.3 = (bf16[48,4096]{1,0:T(8,128)(2,1)S(1)}, bf16[48,4096]{1,0:T(8,128)(2,1)S(1)}, u32[]{:S(2)}, u32[]{:S(2)}) collective-permute-start(bf16[48,4096]{1,0:T(8,128)(2,1)S(1)} %get-tuple-element.26), channel_id=1, source_target_pairs={{0,1},{1,0},{2,3},{3,2},{4,5},{5,4},{6,7},{7,6},{8,9},{9,8},{10,11... | collective-permute-start | bytes 1179656 | tf_op jit(solution)/shard_map/ppermute | solution.py:19
  79.8 23.2 %collective-permute-start.24 = (bf16[24,4096]{1,0:T(8,128)(2,1)S(1)}, bf16[24,4096]{1,0:T(8,128)(2,1)S(1)}, u32[]{:S(2)}, u32[]{:S(2)}) collective-permute-start(bf16[24,4096]{1,0:T(8,128)(2,1)S(1)} %get-tuple-element.40), channel_id=1, source_target_pairs={{0,12},{1,13},{2,14},{3,15},{4,8},{5,9},{6,10},{7,11},{8,4},{9,5},... | collective-permute-start | bytes 589832 | tf_op jit(solution)/shard_map/ppermute | solution.py:19
  82.4 23.7 %collective-permute-start.25 = (bf16[24,4096]{1,0:T(8,128)(2,1)S(1)}, bf16[24,4096]{1,0:T(8,128)(2,1)S(1)}, u32[]{:S(2)}, u32[]{:S(2)}) collective-permute-start(bf16[24,4096]{1,0:T(8,128)(2,1)S(1)} %get-tuple-element.39), channel_id=1, source_target_pairs={{0,14},{1,15},{2,12},{3,13},{4,10},{5,11},{6,8},{7,9},{8,6},{9,7},... | collective-permute-start | bytes 589832 | tf_op jit(solution)/shard_map/ppermute | solution.py:19
  88.3 20.6 %collective-permute-start.17 = (bf16[24,4096]{1,0:T(8,128)(2,1)S(1)}, bf16[24,4096]{1,0:T(8,128)(2,1)S(1)}, u32[]{:S(2)}, u32[]{:S(2)}) collective-permute-start(bf16[24,4096]{1,0:T(8,128)(2,1)S(1)} %get-tuple-element.42), channel_id=1, source_target_pairs={{0,8},{1,9},{2,10},{3,11},{4,12},{5,13},{6,14},{7,15},{8,0},{9,1},... | collective-permute-start | bytes 589832 | tf_op jit(solution)/shard_map/ppermute | solution.py:19
  96.6 14.3 %collective-permute-start.18 = (bf16[24,4096]{1,0:T(8,128)(2,1)S(1)}, bf16[24,4096]{1,0:T(8,128)(2,1)S(1)}, u32[]{:S(2)}, u32[]{:S(2)}) collective-permute-start(bf16[24,4096]{1,0:T(8,128)(2,1)S(1)} %get-tuple-element.41), channel_id=1, source_target_pairs={{0,10},{1,11},{2,8},{3,9},{4,14},{5,15},{6,12},{7,13},{8,2},{9,3},... | collective-permute-start | bytes 589832 | tf_op jit(solution)/shard_map/ppermute | solution.py:19
  102.8 12.3 %collective-permute-start.10 = (bf16[24,4096]{1,0:T(8,128)(2,1)S(1)}, bf16[24,4096]{1,0:T(8,128)(2,1)S(1)}, u32[]{:S(2)}, u32[]{:S(2)}) collective-permute-start(bf16[24,4096]{1,0:T(8,128)(2,1)S(1)} %get-tuple-element.44), channel_id=1, source_target_pairs={{0,4},{1,5},{2,6},{3,7},{4,0},{5,1},{6,2},{7,3},{8,12},{9,13},{10,... | collective-permute-start | bytes 589832 | tf_op jit(solution)/shard_map/ppermute | solution.py:19
  103.0 15.5 %collective-permute-start.11 = (bf16[24,4096]{1,0:T(8,128)(2,1)S(1)}, bf16[24,4096]{1,0:T(8,128)(2,1)S(1)}, u32[]{:S(2)}, u32[]{:S(2)}) collective-permute-start(bf16[24,4096]{1,0:T(8,128)(2,1)S(1)} %get-tuple-element.43), channel_id=1, source_target_pairs={{0,6},{1,7},{2,4},{3,5},{4,2},{5,3},{6,0},{7,1},{8,14},{9,15},{10,... | collective-permute-start | bytes 589832 | tf_op jit(solution)/shard_map/ppermute | solution.py:19
  106.0 12.5 %collective-permute-start.4 = (bf16[24,4096]{1,0:T(8,128)(2,1)S(1)}, bf16[24,4096]{1,0:T(8,128)(2,1)S(1)}, u32[]{:S(2)}, u32[]{:S(2)}) collective-permute-start(bf16[24,4096]{1,0:T(8,128)(2,1)S(1)} %get-tuple-element.45), channel_id=1, source_target_pairs={{0,2},{1,3},{2,0},{3,1},{4,6},{5,7},{6,4},{7,5},{8,10},{9,11},{10,... | collective-permute-start | bytes 589832 | tf_op jit(solution)/shard_map/ppermute | solution.py:19

commit v4 on v3

--- a/solution.py
+++ b/solution.py
@@ -95,29 +95,29 @@
     return blocks, table
 
 
-def combine_kernel(tokens, table, *refs):
-    blocks, out, rows = refs[:EXPERTS], refs[EXPERTS], refs[EXPERTS + 1]
-    for r in range(EXPERTS):
-        rows[pl.ds(r * CAP, CAP), :] = blocks[r][...]
-    share = table[...].T
+def combine_kernel(picked, base, table, *refs):
+    blocks, out, rows = refs[:-2], refs[-2], refs[-1]
+    for i, ref in enumerate(blocks):
+        rows[pl.ds(i * CAP, CAP), :] = ref[...]
+    share = jnp.concatenate([table[r * CAP:(r + 1) * CAP, :] for r in picked], axis=0).T
     high = share.astype(jnp.bfloat16)
     low = (share - high.astype(jnp.float32)).astype(jnp.bfloat16)
     mixture = jnp.dot(high, rows[...], preferred_element_type=jnp.float32)
     mixture = mixture + jnp.dot(low, rows[...], preferred_element_type=jnp.float32)
-    out[...] = (tokens[...].astype(jnp.float32) + mixture).astype(jnp.bfloat16)
+    out[...] = (base[...].astype(jnp.float32) + mixture).astype(out.dtype)
 
 
-def combine(tokens, table, blocks):
-    count, width = tokens.shape
+def combine(base, table, blocks, picked, kind):
+    count, width = base.shape
     return pl.pallas_call(
-        combine_kernel,
-        out_shape=jax.ShapeDtypeStruct((count, width), jnp.bfloat16),
-        in_specs=[VMEM] * (EXPERTS + 2),
+        lambda *refs: combine_kernel(picked, *refs),
+        out_shape=jax.ShapeDtypeStruct((count, width), kind),
+        in_specs=[VMEM] * (len(picked) + 2),
         out_specs=VMEM,
-        scratch_shapes=[pltpu.VMEM((EXPERTS * CAP, width), jnp.bfloat16)],
-        cost_estimate=pl.CostEstimate(flops=4 * count * EXPERTS * CAP * width, bytes_accessed=4 * count * width, transcendentals=0),
+        scratch_shapes=[pltpu.VMEM((len(picked) * CAP, width), jnp.bfloat16)],
+        cost_estimate=pl.CostEstimate(flops=4 * count * len(picked) * CAP * width, bytes_accessed=4 * count * width, transcendentals=0),
         compiler_params=pltpu.CompilerParams(vmem_limit_bytes=12 << 20),
-    )(tokens, table, *blocks)
+    )(base, table, *[blocks[r] for r in picked])
 
 
 def experts(own, others, w_gate, w_up, w_down):
@@ -157,7 +157,8 @@
         for i, r in enumerate(rs):
             done = summed[i * CAP:(i + 1) * CAP].astype(jnp.bfloat16)
             back[r] = flip(done, r * shards, n_devices)
-    return combine(tokens, table, back)
+    early = combine(tokens, table, back, (2, 3, 4, 5), jnp.float32)
+    return combine(early, table, back, (6, 7, 0, 1), tokens.dtype)
 
 
 def solution(mesh):

time: 120 us -> 126 us (1.050)
  starting transfers between devices: 50.3 us -> 55.3 us
    ppermute x26, starting transfers between devices: 50.3 us -> 55.3 us  [flip(): lax.ppermute(values, 'expert', [(i, i ^ mask) for i in range(n_devices)])]
  transfers between devices with their start and end apart: 26 -> 26, of which waited for: 17 -> 12; matrix products, arithmetic and copies ran while one was open for 0% -> 0% of each run, Pallas kernels for 14% -> 14%
where the time goes in v4:
time: 126 us
  starting transfers between devices  55.3 us (44%)
  waiting for transfers between devices  49.1 us (39%)
  Pallas kernels  20.9 us (17%)
    ppermute x26, starting transfers between devices, flip(): lax.ppermute(values, 'expert', [(i, i ^ mask) for i in range(n_devices)])  55.3 us
    ppermute x26, waiting for transfers between devices, flip(): lax.ppermute(values, 'expert', [(i, i ^ mask) for i in range(n_devices)])  49.1 us
    pallas_call x4, Pallas kernels, experts(): pl.pallas_call(lambda *refs: expert_kernel(blocks, *refs), out_shape=(jax...  17 us
  transfers between devices with their start and end apart: 26, of which 12 were waited for; matrix products, arithmetic and copies ran while one was open for 0% of the time, Pallas kernels for 14%

profile of v4, /device:TPU:0, one launch (start us, length us, event | category | flops | bytes accessed | tf_op | source)
XLA Modules:
  0.0 126.0 jit_solution(11258866811382429160)
XLA Ops:
  0.0 2.2 %shard_map.73 = (bf16[24,4096]{1,0:T(8,128)(2,1)S(1)}, bf16[24,4096]{1,0:T(8,128)(2,1)S(1)}, bf16[24,4096]{1,0:T(8,128)(2,1)S(1)}, bf16[24,4096]{1,0:T(8,128)(2,...) custom-call(s32[1]{0:T(128)} %bitcast.own_expert, ...), custom_call_target="tpu_custom_call" | custom-call | flops 20000000000 | bytes 1048576 | tf_op jit(solution)/shard_map/pallas_call | solution.py:85
  2.2 3.1 %collective-permute-start.21 = (bf16[24,4096]{1,0:T(8,128)(2,1)S(1)}, bf16[24,4096]{1,0:T(8,128)(2,1)S(1)}, u32[]{:S(2)}, u32[]{:S(2)}) collective-permute-start(bf16[24,4096]{1,0:T(8,128)(2,1)S(1)} %get-tuple-element.36), channel_id=1, source_target_pairs={{0,2},{1,3},{2,0},{3,1},{4,6},{5,7},{6,4},{7,5},{8,10},{9,11},{10,... | collective-permute-start | bytes 589832 | tf_op jit(solution)/shard_map/ppermute | solution.py:19
  5.2 1.5 %collective-permute-start.22 = (bf16[24,4096]{1,0:T(8,128)(2,1)S(1)}, bf16[24,4096]{1,0:T(8,128)(2,1)S(1)}, u32[]{:S(2)}, u32[]{:S(2)}) collective-permute-start(bf16[24,4096]{1,0:T(8,128)(2,1)S(1)} %get-tuple-element.35.refs_0_), channel_id=1, source_target_pairs={{0,1},{1,0},{2,3},{3,2},{4,5},{5,4},{6,7},{7,6},{8,9},{9,8},{10,11... | collective-permute-start | bytes 589832 | tf_op jit(solution)/shard_map/ppermute | solution.py:19
  6.7 3.6 %collective-permute-start.14 = (bf16[24,4096]{1,0:T(8,128)(2,1)S(1)}, bf16[24,4096]{1,0:T(8,128)(2,1)S(1)}, u32[]{:S(2)}, u32[]{:S(2)}) collective-permute-start(bf16[24,4096]{1,0:T(8,128)(2,1)S(1)} %get-tuple-element.31), channel_id=1, source_target_pairs={{0,12},{1,13},{2,14},{3,15},{4,8},{5,9},{6,10},{7,11},{8,4},{9,5},... | collective-permute-start | bytes 589832 | tf_op jit(solution)/shard_map/ppermute | solution.py:19
  10.3 0.2 collective-permute-start.15
  10.5 1.7 %collective-permute-start.8 = (bf16[24,4096]{1,0:T(8,128)(2,1)S(1)}, bf16[24,4096]{1,0:T(8,128)(2,1)S(1)}, u32[]{:S(2)}, u32[]{:S(2)}) collective-permute-start(bf16[24,4096]{1,0:T(8,128)(2,1)S(1)} %get-tuple-element.28), channel_id=1, source_target_pairs={{0,10},{1,11},{2,8},{3,9},{4,14},{5,15},{6,12},{7,13},{8,2},{9,3},... | collective-permute-start | bytes 589832 | tf_op jit(solution)/shard_map/ppermute | solution.py:19
  12.3 0.5 collective-permute-start.23
  12.8 2.1 %collective-permute-start.7 = (bf16[24,4096]{1,0:T(8,128)(2,1)S(1)}, bf16[24,4096]{1,0:T(8,128)(2,1)S(1)}, u32[]{:S(2)}, u32[]{:S(2)}) collective-permute-start(bf16[24,4096]{1,0:T(8,128)(2,1)S(1)} %get-tuple-element.27), channel_id=1, source_target_pairs={{0,8},{1,9},{2,10},{3,11},{4,12},{5,13},{6,14},{7,15},{8,0},{9,1},... | collective-permute-start | bytes 589832 | tf_op jit(solution)/shard_map/ppermute | solution.py:19
  14.9 0.9 collective-permute-done.14.refs_0_
  15.8 16.4 %collective-permute-start = (bf16[24,4096]{1,0:T(8,128)(2,1)S(1)}, bf16[24,4096]{1,0:T(8,128)(2,1)S(1)}, u32[]{:S(2)}, u32[]{:S(2)}) collective-permute-start(bf16[24,4096]{1,0:T(8,128)(2,1)S(1)} %get-tuple-element.23), channel_id=1, source_target_pairs={{0,4},{1,5},{2,6},{3,7},{4,0},{5,1},{6,2},{7,3},{8,12},{9,13},{10,... | collective-permute-start | bytes 589832 | tf_op jit(solution)/shard_map/ppermute | solution.py:19
  32.2 5.1 %collective-permute-start.1 = (bf16[24,4096]{1,0:T(8,128)(2,1)S(1)}, bf16[24,4096]{1,0:T(8,128)(2,1)S(1)}, u32[]{:S(2)}, u32[]{:S(2)}) collective-permute-start(bf16[24,4096]{1,0:T(8,128)(2,1)S(1)} %get-tuple-element.24), channel_id=1, source_target_pairs={{0,6},{1,7},{2,4},{3,5},{4,2},{5,3},{6,0},{7,1},{8,14},{9,15},{10,... | collective-permute-start | bytes 589832 | tf_op jit(solution)/shard_map/ppermute | solution.py:19
  37.3 2.8 %collective-permute-done.8.refs_1_ = bf16[24,4096]{1,0:T(8,128)(2,1)S(1)} collective-permute-done((bf16[24,4096]{1,0:T(8,128)(2,1)S(1)}, bf16[24,4096]{1,0:T(8,128)(2,1)S(1)}, u32[]{:S(2)}, u32[]{:S(2)}) %collective-permute-start.8) | collective-permute-done | bytes 196640 | tf_op jit(solution)/shard_map/ppermute | solution.py:19
  40.1 0.5 collective-permute-start.16
  40.6 1.5 %collective-permute-start.17 = (bf16[24,4096]{1,0:T(8,128)(2,1)S(1)}, bf16[24,4096]{1,0:T(8,128)(2,1)S(1)}, u32[]{:S(2)}, u32[]{:S(2)}) collective-permute-start(bf16[24,4096]{1,0:T(8,128)(2,1)S(1)} %collective-permute-done.15.refs_1_), channel_id=1, source_target_pairs={{0,1},{1,0},{2,3},{3,2},{4,5},{5,4},{6,7},{7,6},{8,9},{9,8},{10,11... | collective-permute-start | bytes 589832 | tf_op jit(solution)/shard_map/ppermute | solution.py:19
  42.1 4.2 %shard_map.78 = (f32[48,4096]{1,0:T(8,128)S(1)}, bf16[48,4096]{1,0:T(8,128)(2,1)S(1)}) custom-call(bf16[24,4096]{1,0:T(8,128)(2,1)S(1)} %get-tuple-element.35.refs_0_, bf16[24,4096]{1,0:T(8,128)(2,1)S(1)} %collective-permute-done.21.refs_1_, bf16[24,4096]{1,0:T(8,128)(2,1)S(1)} %collective-permute-done.22.refs_2_, ...), custom_call_target="tpu_custom_call" | custom-call | flops 4227858432 | bytes 22020096 | tf_op jit(solution)/shard_map/pallas_call | solution.py:128
  46.4 0.6 collective-permute-start.10
  47.0 1.5 %collective-permute-start.9 = (bf16[24,4096]{1,0:T(8,128)(2,1)S(1)}, bf16[24,4096]{1,0:T(8,128)(2,1)S(1)}, u32[]{:S(2)}, u32[]{:S(2)}) collective-permute-start(bf16[24,4096]{1,0:T(8,128)(2,1)S(1)} %collective-permute-done.7.refs_0_), channel_id=1, source_target_pairs={{0,1},{1,0},{2,3},{3,2},{4,5},{5,4},{6,7},{7,6},{8,9},{9,8},{10,11... | collective-permute-start | bytes 589832 | tf_op jit(solution)/shard_map/ppermute | solution.py:19
  48.5 0.5 collective-permute-start.2
  49.0 1.5 %collective-permute-start.3 = (bf16[24,4096]{1,0:T(8,128)(2,1)S(1)}, bf16[24,4096]{1,0:T(8,128)(2,1)S(1)}, u32[]{:S(2)}, u32[]{:S(2)}) collective-permute-start(bf16[24,4096]{1,0:T(8,128)(2,1)S(1)} %collective-permute-done.1.refs_1_), channel_id=1, source_target_pairs={{0,1},{1,0},{2,3},{3,2},{4,5},{5,4},{6,7},{7,6},{8,9},{9,8},{10,11... | collective-permute-start | bytes 589832 | tf_op jit(solution)/shard_map/ppermute | solution.py:19
  50.5 1.5 %collective-permute-done.17.refs_3_ = bf16[24,4096]{1,0:T(8,128)(2,1)S(1)} collective-permute-done((bf16[24,4096]{1,0:T(8,128)(2,1)S(1)}, bf16[24,4096]{1,0:T(8,128)(2,1)S(1)}, u32[]{:S(2)}, u32[]{:S(2)}) %collective-permute-start.17) | collective-permute-done | bytes 196640 | tf_op jit(solution)/shard_map/ppermute | solution.py:19
  51.9 0.5 collective-permute-start.24
  52.5 4.2 %shard_map.77 = (f32[48,4096]{1,0:T(8,128)S(1)}, bf16[48,4096]{1,0:T(8,128)(2,1)S(1)}) custom-call(bf16[24,4096]{1,0:T(8,128)(2,1)S(1)} %collective-permute-done.14.refs_0_, bf16[24,4096]{1,0:T(8,128)(2,1)S(1)} %collective-permute-done.15.refs_1_, bf16[24,4096]{1,0:T(8,128)(2,1)S(1)} %collective-permute-done.16.refs_2_, ...), custom_call_target="tpu_custom_call" | custom-call | flops 4227858432 | bytes 22020096 | tf_op jit(solution)/shard_map/pallas_call | solution.py:128
  56.7 1.6 %collective-permute-start.18 = (bf16[48,4096]{1,0:T(8,128)(2,1)S(1)}, bf16[48,4096]{1,0:T(8,128)(2,1)S(1)}, u32[]{:S(2)}, u32[]{:S(2)}) collective-permute-start(bf16[48,4096]{1,0:T(8,128)(2,1)S(1)} %get-tuple-element.34), channel_id=1, source_target_pairs={{0,1},{1,0},{2,3},{3,2},{4,5},{5,4},{6,7},{7,6},{8,9},{9,8},{10,11... | collective-permute-start | bytes 1179656 | tf_op jit(solution)/shard_map/ppermute | solution.py:19
  58.3 2.1 %collective-permute-done.9.refs_2_ = bf16[24,4096]{1,0:T(8,128)(2,1)S(1)} collective-permute-done((bf16[24,4096]{1,0:T(8,128)(2,1)S(1)}, bf16[24,4096]{1,0:T(8,128)(2,1)S(1)}, u32[]{:S(2)}, u32[]{:S(2)}) %collective-permute-start.9) | collective-permute-done | bytes 196640 | tf_op jit(solution)/shard_map/ppermute | solution.py:19
  60.4 4.4 %shard_map.75 = (f32[48,4096]{1,0:T(8,128)S(1)}, bf16[48,4096]{1,0:T(8,128)(2,1)S(1)}) custom-call(bf16[24,4096]{1,0:T(8,128)(2,1)S(1)} %collective-permute-done.7.refs_0_, bf16[24,4096]{1,0:T(8,128)(2,1)S(1)} %collective-permute-done.8.refs_1_, bf16[24,4096]{1,0:T(8,128)(2,1)S(1)} %collective-permute-done.9.refs_2_, ...), custom_call_target="tpu_custom_call" | custom-call | flops 4227858432 | bytes 22020096 | tf_op jit(solution)/shard_map/pallas_call | solution.py:128
  64.8 0.6 collective-permute-start.11
  65.4 3.4 %collective-permute-done.3.refs_3_ = bf16[24,4096]{1,0:T(8,128)(2,1)S(1)} collective-permute-done((bf16[24,4096]{1,0:T(8,128)(2,1)S(1)}, bf16[24,4096]{1,0:T(8,128)(2,1)S(1)}, u32[]{:S(2)}, u32[]{:S(2)}) %collective-permute-start.3) | collective-permute-done | bytes 196640 | tf_op jit(solution)/shard_map/ppermute | solution.py:19
  68.8 4.2 %shard_map.74 = (f32[48,4096]{1,0:T(8,128)S(1)}, bf16[48,4096]{1,0:T(8,128)(2,1)S(1)}) custom-call(bf16[24,4096]{1,0:T(8,128)(2,1)S(1)} %collective-permute-done.refs_0_, bf16[24,4096]{1,0:T(8,128)(2,1)S(1)} %collective-permute-done.1.refs_1_, bf16[24,4096]{1,0:T(8,128)(2,1)S(1)} %collective-permute-done.2.refs_2_, ...), custom_call_target="tpu_custom_call" | custom-call | flops 4227858432 | bytes 22020096 | tf_op jit(solution)/shard_map/pallas_call | solution.py:128
  73.0 0.6 collective-permute-start.4
  73.6 3.6 %collective-permute-done.24 = bf16[48,4096]{1,0:T(8,128)(2,1)S(1)} collective-permute-done((bf16[48,4096]{1,0:T(8,128)(2,1)S(1)}, bf16[48,4096]{1,0:T(8,128)(2,1)S(1)}, u32[]{:S(2)}, u32[]{:S(2)}) %collective-permute-start.24) | collective-permute-done | bytes 393248 | tf_op jit(solution)/shard_map/ppermute | solution.py:19
  77.2 0.1 add_convert_fusion
  77.3 1.6 %collective-permute-start.25 = (bf16[24,4096]{1,0:T(8,128)(2,1)S(1)}, bf16[24,4096]{1,0:T(8,128)(2,1)S(1)}, u32[]{:S(2)}, u32[]{:S(2)}) collective-permute-start(bf16[24,4096]{1,0:T(8,128)(2,1)S(1)} %get-tuple-element.39), channel_id=1, source_target_pairs={{0,2},{1,3},{2,0},{3,1},{4,6},{5,7},{6,4},{7,5},{8,10},{9,11},{10,... | collective-permute-start | bytes 589832 | tf_op jit(solution)/shard_map/ppermute | solution.py:19
  78.9 15.2 %collective-permute-done.11 = bf16[48,4096]{1,0:T(8,128)(2,1)S(1)} collective-permute-done((bf16[48,4096]{1,0:T(8,128)(2,1)S(1)}, bf16[48,4096]{1,0:T(8,128)(2,1)S(1)}, u32[]{:S(2)}, u32[]{:S(2)}) %collective-permute-start.11) | collective-permute-done | bytes 393248 | tf_op jit(solution)/shard_map/ppermute | solution.py:19
  94.1 0.1 add_convert_fusion.2
  94.2 0.1 collective-permute-start.12
  94.3 3.9 %collective-permute-start.13 = (bf16[24,4096]{1,0:T(8,128)(2,1)S(1)}, bf16[24,4096]{1,0:T(8,128)(2,1)S(1)}, u32[]{:S(2)}, u32[]{:S(2)}) collective-permute-start(bf16[24,4096]{1,0:T(8,128)(2,1)S(1)} %get-tuple-element.43), channel_id=1, source_target_pairs={{0,10},{1,11},{2,8},{3,9},{4,14},{5,15},{6,12},{7,13},{8,2},{9,3},... | collective-permute-start | bytes 589832 | tf_op jit(solution)/shard_map/ppermute | solution.py:19
  98.1 1.7 %collective-permute-done.4 = bf16[48,4096]{1,0:T(8,128)(2,1)S(1)} collective-permute-done((bf16[48,4096]{1,0:T(8,128)(2,1)S(1)}, bf16[48,4096]{1,0:T(8,128)(2,1)S(1)}, u32[]{:S(2)}, u32[]{:S(2)}) %collective-permute-start.4) | collective-permute-done | bytes 393248 | tf_op jit(solution)/shard_map/ppermute | solution.py:19
  99.8 0.1 add_convert_fusion.3
  100.0 0.1 collective-permute-start.5
  100.1 3.0 %collective-permute-start.6 = (bf16[24,4096]{1,0:T(8,128)(2,1)S(1)}, bf16[24,4096]{1,0:T(8,128)(2,1)S(1)}, u32[]{:S(2)}, u32[]{:S(2)}) collective-permute-start(bf16[24,4096]{1,0:T(8,128)(2,1)S(1)} %get-tuple-element.45), channel_id=1, source_target_pairs={{0,6},{1,7},{2,4},{3,5},{4,2},{5,3},{6,0},{7,1},{8,14},{9,15},{10,... | collective-permute-start | bytes 589832 | tf_op jit(solution)/shard_map/ppermute | solution.py:19
  103.1 3.1 %collective-permute-done.12.refs_4_ = bf16[24,4096]{1,0:T(8,128)(2,1)S(1)} collective-permute-done((bf16[24,4096]{1,0:T(8,128)(2,1)S(1)}, bf16[24,4096]{1,0:T(8,128)(2,1)S(1)}, u32[]{:S(2)}, u32[]{:S(2)}) %collective-permute-start.12) | collective-permute-done | bytes 196640 | tf_op jit(solution)/shard_map/ppermute | solution.py:19
  106.3 1.8 %collective-permute-start.19 = (bf16[24,4096]{1,0:T(8,128)(2,1)S(1)}, bf16[24,4096]{1,0:T(8,128)(2,1)S(1)}, u32[]{:S(2)}, u32[]{:S(2)}) collective-permute-start(bf16[24,4096]{1,0:T(8,128)(2,1)S(1)} %get-tuple-element.42), channel_id=1, source_target_pairs={{0,12},{1,13},{2,14},{3,15},{4,8},{5,9},{6,10},{7,11},{8,4},{9,5},... | collective-permute-start | bytes 589832 | tf_op jit(solution)/shard_map/ppermute | solution.py:19
  108.1 5.9 %collective-permute-done.13.refs_5_ = bf16[24,4096]{1,0:T(8,128)(2,1)S(1)} collective-permute-done((bf16[24,4096]{1,0:T(8,128)(2,1)S(1)}, bf16[24,4096]{1,0:T(8,128)(2,1)S(1)}, u32[]{:S(2)}, u32[]{:S(2)}) %collective-permute-start.13) | collective-permute-done | bytes 196640 | tf_op jit(solution)/shard_map/ppermute | solution.py:19
  114.0 1.3 %collective-permute-start.20 = (bf16[24,4096]{1,0:T(8,128)(2,1)S(1)}, bf16[24,4096]{1,0:T(8,128)(2,1)S(1)}, u32[]{:S(2)}, u32[]{:S(2)}) collective-permute-start(bf16[24,4096]{1,0:T(8,128)(2,1)S(1)} %get-tuple-element.41), channel_id=1, source_target_pairs={{0,14},{1,15},{2,12},{3,13},{4,10},{5,11},{6,8},{7,9},{8,6},{9,7},... | collective-permute-start | bytes 589832 | tf_op jit(solution)/shard_map/ppermute | solution.py:19
  115.4 2.5 %collective-permute-done.5.refs_2_ = bf16[24,4096]{1,0:T(8,128)(2,1)S(1)} collective-permute-done((bf16[24,4096]{1,0:T(8,128)(2,1)S(1)}, bf16[24,4096]{1,0:T(8,128)(2,1)S(1)}, u32[]{:S(2)}, u32[]{:S(2)}) %collective-permute-start.5) | collective-permute-done | bytes 196640 | tf_op jit(solution)/shard_map/ppermute | solution.py:19
  117.9 6.3 %collective-permute-done.6.refs_3_ = bf16[24,4096]{1,0:T(8,128)(2,1)S(1)} collective-permute-done((bf16[24,4096]{1,0:T(8,128)(2,1)S(1)}, bf16[24,4096]{1,0:T(8,128)(2,1)S(1)}, u32[]{:S(2)}, u32[]{:S(2)}) %collective-permute-start.6) | collective-permute-done | bytes 196640 | tf_op jit(solution)/shard_map/ppermute | solution.py:19
  124.2 0.5 shard_map.76.refs_0_
  124.7 1.3 %shard_map.79 = bf16[64,4096]{1,0:T(8,128)(2,1)} custom-call(f32[64,4096]{1,0:T(8,128)S(1)} %shard_map.76.refs_0_, f32[192,64]{1,0:T(8,128)S(1)} %get-tuple-element.22.refs_1_, bf16[24,4096]{1,0:T(8,128)(2,1)S(1)} %collective-permute-done.19.refs_2_, bf16[24,4096]{1,0:T(8,128)(2,1)S(1)} %collective-permute-done.20.refs_3_, ...), custom_call_target="tpu_custom_call" | custom-call | flops 100663296 | bytes 1048576 | tf_op jit(solution)/shard_map/pallas_call | solution.py:112
  (27 shorter events, 0.2 us)
Async XLA Ops:
  0.0 42.1 %copy-start = (bf16[1,4096,896]{2,1,0:T(8,128)(2,1)S(1)}, bf16[1,4096,896]{2,1,0:T(8,128)(2,1)}, u32[]{:S(2)}) copy-start(bf16[1,4096,896]{2,1,0:T(8,128)(2,1)} %refs_4_.7) | copy-start | bytes 22020100
  0.0 42.1 %copy-start.1 = (bf16[1,4096,896]{2,1,0:T(8,128)(2,1)S(1)}, bf16[1,4096,896]{2,1,0:T(8,128)(2,1)}, u32[]{:S(2)}) copy-start(bf16[1,4096,896]{2,1,0:T(8,128)(2,1)} %refs_5_.7) | copy-start | bytes 22020100
  0.0 42.1 %copy-start.2 = (bf16[1,896,4096]{2,1,0:T(8,128)(2,1)S(1)}, bf16[1,896,4096]{2,1,0:T(8,128)(2,1)}, u32[]{:S(2)}) copy-start(bf16[1,896,4096]{2,1,0:T(8,128)(2,1)} %refs_6_.7) | copy-start | bytes 22020100
  2.2 10.1 %collective-permute-start.21 = (bf16[24,4096]{1,0:T(8,128)(2,1)S(1)}, bf16[24,4096]{1,0:T(8,128)(2,1)S(1)}, u32[]{:S(2)}, u32[]{:S(2)}) collective-permute-start(bf16[24,4096]{1,0:T(8,128)(2,1)S(1)} %get-tuple-element.36), channel_id=1, source_target_pairs={{0,2},{1,3},{2,0},{3,1},{4,6},{5,7},{6,4},{7,5},{8,10},{9,11},{10,... | collective-permute-start | bytes 589832 | tf_op jit(solution)/shard_map/ppermute | solution.py:19
  5.2 7.5 %collective-permute-start.22 = (bf16[24,4096]{1,0:T(8,128)(2,1)S(1)}, bf16[24,4096]{1,0:T(8,128)(2,1)S(1)}, u32[]{:S(2)}, u32[]{:S(2)}) collective-permute-start(bf16[24,4096]{1,0:T(8,128)(2,1)S(1)} %get-tuple-element.35.refs_0_), channel_id=1, source_target_pairs={{0,1},{1,0},{2,3},{3,2},{4,5},{5,4},{6,7},{7,6},{8,9},{9,8},{10,11... | collective-permute-start | bytes 589832 | tf_op jit(solution)/shard_map/ppermute | solution.py:19
  6.7 9.1 %collective-permute-start.14 = (bf16[24,4096]{1,0:T(8,128)(2,1)S(1)}, bf16[24,4096]{1,0:T(8,128)(2,1)S(1)}, u32[]{:S(2)}, u32[]{:S(2)}) collective-permute-start(bf16[24,4096]{1,0:T(8,128)(2,1)S(1)} %get-tuple-element.31), channel_id=1, source_target_pairs={{0,12},{1,13},{2,14},{3,15},{4,8},{5,9},{6,10},{7,11},{8,4},{9,5},... | collective-permute-start | bytes 589832 | tf_op jit(solution)/shard_map/ppermute | solution.py:19
  10.3 21.9 %collective-permute-start.15 = (bf16[24,4096]{1,0:T(8,128)(2,1)S(1)}, bf16[24,4096]{1,0:T(8,128)(2,1)S(1)}, u32[]{:S(2)}, u32[]{:S(2)}) collective-permute-start(bf16[24,4096]{1,0:T(8,128)(2,1)S(1)} %get-tuple-element.32), channel_id=1, source_target_pairs={{0,14},{1,15},{2,12},{3,13},{4,10},{5,11},{6,8},{7,9},{8,6},{9,7},... | collective-permute-start | bytes 589832 | tf_op jit(solution)/shard_map/ppermute | solution.py:19
  10.5 29.6 %collective-permute-start.8 = (bf16[24,4096]{1,0:T(8,128)(2,1)S(1)}, bf16[24,4096]{1,0:T(8,128)(2,1)S(1)}, u32[]{:S(2)}, u32[]{:S(2)}) collective-permute-start(bf16[24,4096]{1,0:T(8,128)(2,1)S(1)} %get-tuple-element.28), channel_id=1, source_target_pairs={{0,10},{1,11},{2,8},{3,9},{4,14},{5,15},{6,12},{7,13},{8,2},{9,3},... | collective-permute-start | bytes 589832 | tf_op jit(solution)/shard_map/ppermute | solution.py:19
  12.3 28.4 %collective-permute-start.23 = (bf16[24,4096]{1,0:T(8,128)(2,1)S(1)}, bf16[24,4096]{1,0:T(8,128)(2,1)S(1)}, u32[]{:S(2)}, u32[]{:S(2)}) collective-permute-start(bf16[24,4096]{1,0:T(8,128)(2,1)S(1)} %collective-permute-done.21.refs_1_), channel_id=1, source_target_pairs={{0,1},{1,0},{2,3},{3,2},{4,5},{5,4},{6,7},{7,6},{8,9},{9,8},{10,11... | collective-permute-start | bytes 589832 | tf_op jit(solution)/shard_map/ppermute | solution.py:19
  12.8 33.6 %collective-permute-start.7 = (bf16[24,4096]{1,0:T(8,128)(2,1)S(1)}, bf16[24,4096]{1,0:T(8,128)(2,1)S(1)}, u32[]{:S(2)}, u32[]{:S(2)}) collective-permute-start(bf16[24,4096]{1,0:T(8,128)(2,1)S(1)} %get-tuple-element.27), channel_id=1, source_target_pairs={{0,8},{1,9},{2,10},{3,11},{4,12},{5,13},{6,14},{7,15},{8,0},{9,1},... | collective-permute-start | bytes 589832 | tf_op jit(solution)/shard_map/ppermute | solution.py:19
  15.8 31.1 %collective-permute-start = (bf16[24,4096]{1,0:T(8,128)(2,1)S(1)}, bf16[24,4096]{1,0:T(8,128)(2,1)S(1)}, u32[]{:S(2)}, u32[]{:S(2)}) collective-permute-start(bf16[24,4096]{1,0:T(8,128)(2,1)S(1)} %get-tuple-element.23), channel_id=1, source_target_pairs={{0,4},{1,5},{2,6},{3,7},{4,0},{5,1},{6,2},{7,3},{8,12},{9,13},{10,... | collective-permute-start | bytes 589832 | tf_op jit(solution)/shard_map/ppermute | solution.py:19
  32.2 16.3 %collective-permute-start.1 = (bf16[24,4096]{1,0:T(8,128)(2,1)S(1)}, bf16[24,4096]{1,0:T(8,128)(2,1)S(1)}, u32[]{:S(2)}, u32[]{:S(2)}) collective-permute-start(bf16[24,4096]{1,0:T(8,128)(2,1)S(1)} %get-tuple-element.24), channel_id=1, source_target_pairs={{0,6},{1,7},{2,4},{3,5},{4,2},{5,3},{6,0},{7,1},{8,14},{9,15},{10,... | collective-permute-start | bytes 589832 | tf_op jit(solution)/shard_map/ppermute | solution.py:19
  40.1 8.9 %collective-permute-start.16 = (bf16[24,4096]{1,0:T(8,128)(2,1)S(1)}, bf16[24,4096]{1,0:T(8,128)(2,1)S(1)}, u32[]{:S(2)}, u32[]{:S(2)}) collective-permute-start(bf16[24,4096]{1,0:T(8,128)(2,1)S(1)} %collective-permute-done.14.refs_0_), channel_id=1, source_target_pairs={{0,1},{1,0},{2,3},{3,2},{4,5},{5,4},{6,7},{7,6},{8,9},{9,8},{10,11... | collective-permute-start | bytes 589832 | tf_op jit(solution)/shard_map/ppermute | solution.py:19
  40.6 11.3 %collective-permute-start.17 = (bf16[24,4096]{1,0:T(8,128)(2,1)S(1)}, bf16[24,4096]{1,0:T(8,128)(2,1)S(1)}, u32[]{:S(2)}, u32[]{:S(2)}) collective-permute-start(bf16[24,4096]{1,0:T(8,128)(2,1)S(1)} %collective-permute-done.15.refs_1_), channel_id=1, source_target_pairs={{0,1},{1,0},{2,3},{3,2},{4,5},{5,4},{6,7},{7,6},{8,9},{9,8},{10,11... | collective-permute-start | bytes 589832 | tf_op jit(solution)/shard_map/ppermute | solution.py:19
  46.4 10.3 %collective-permute-start.10 = (bf16[24,4096]{1,0:T(8,128)(2,1)S(1)}, bf16[24,4096]{1,0:T(8,128)(2,1)S(1)}, u32[]{:S(2)}, u32[]{:S(2)}) collective-permute-start(bf16[24,4096]{1,0:T(8,128)(2,1)S(1)} %collective-permute-done.8.refs_1_), channel_id=1, source_target_pairs={{0,1},{1,0},{2,3},{3,2},{4,5},{5,4},{6,7},{7,6},{8,9},{9,8},{10,11... | collective-permute-start | bytes 589832 | tf_op jit(solution)/shard_map/ppermute | solution.py:19
  47.0 13.4 %collective-permute-start.9 = (bf16[24,4096]{1,0:T(8,128)(2,1)S(1)}, bf16[24,4096]{1,0:T(8,128)(2,1)S(1)}, u32[]{:S(2)}, u32[]{:S(2)}) collective-permute-start(bf16[24,4096]{1,0:T(8,128)(2,1)S(1)} %collective-permute-done.7.refs_0_), channel_id=1, source_target_pairs={{0,1},{1,0},{2,3},{3,2},{4,5},{5,4},{6,7},{7,6},{8,9},{9,8},{10,11... | collective-permute-start | bytes 589832 | tf_op jit(solution)/shard_map/ppermute | solution.py:19
  48.5 16.9 %collective-permute-start.2 = (bf16[24,4096]{1,0:T(8,128)(2,1)S(1)}, bf16[24,4096]{1,0:T(8,128)(2,1)S(1)}, u32[]{:S(2)}, u32[]{:S(2)}) collective-permute-start(bf16[24,4096]{1,0:T(8,128)(2,1)S(1)} %collective-permute-done.refs_0_), channel_id=1, source_target_pairs={{0,1},{1,0},{2,3},{3,2},{4,5},{5,4},{6,7},{7,6},{8,9},{9,8},{10,11... | collective-permute-start | bytes 589832 | tf_op jit(solution)/shard_map/ppermute | solution.py:19
  49.0 19.8 %collective-permute-start.3 = (bf16[24,4096]{1,0:T(8,128)(2,1)S(1)}, bf16[24,4096]{1,0:T(8,128)(2,1)S(1)}, u32[]{:S(2)}, u32[]{:S(2)}) collective-permute-start(bf16[24,4096]{1,0:T(8,128)(2,1)S(1)} %collective-permute-done.1.refs_1_), channel_id=1, source_target_pairs={{0,1},{1,0},{2,3},{3,2},{4,5},{5,4},{6,7},{7,6},{8,9},{9,8},{10,11... | collective-permute-start | bytes 589832 | tf_op jit(solution)/shard_map/ppermute | solution.py:19
  51.9 25.3 %collective-permute-start.24 = (bf16[48,4096]{1,0:T(8,128)(2,1)S(1)}, bf16[48,4096]{1,0:T(8,128)(2,1)S(1)}, u32[]{:S(2)}, u32[]{:S(2)}) collective-permute-start(bf16[48,4096]{1,0:T(8,128)(2,1)S(1)} %get-tuple-element.38), channel_id=1, source_target_pairs={{0,1},{1,0},{2,3},{3,2},{4,5},{5,4},{6,7},{7,6},{8,9},{9,8},{10,11... | collective-permute-start | bytes 1179656 | tf_op jit(solution)/shard_map/ppermute | solution.py:19
  56.7 43.4 %collective-permute-start.18 = (bf16[48,4096]{1,0:T(8,128)(2,1)S(1)}, bf16[48,4096]{1,0:T(8,128)(2,1)S(1)}, u32[]{:S(2)}, u32[]{:S(2)}) collective-permute-start(bf16[48,4096]{1,0:T(8,128)(2,1)S(1)} %get-tuple-element.34), channel_id=1, source_target_pairs={{0,1},{1,0},{2,3},{3,2},{4,5},{5,4},{6,7},{7,6},{8,9},{9,8},{10,11... | collective-permute-start | bytes 1179656 | tf_op jit(solution)/shard_map/ppermute | solution.py:19
  64.8 29.3 %collective-permute-start.11 = (bf16[48,4096]{1,0:T(8,128)(2,1)S(1)}, bf16[48,4096]{1,0:T(8,128)(2,1)S(1)}, u32[]{:S(2)}, u32[]{:S(2)}) collective-permute-start(bf16[48,4096]{1,0:T(8,128)(2,1)S(1)} %get-tuple-element.30), channel_id=1, source_target_pairs={{0,1},{1,0},{2,3},{3,2},{4,5},{5,4},{6,7},{7,6},{8,9},{9,8},{10,11... | collective-permute-start | bytes 1179656 | tf_op jit(solution)/shard_map/ppermute | solution.py:19
  73.0 51.2 %copy-start.3 = (bf16[64,4096]{1,0:T(8,128)(2,1)S(1)}, bf16[64,4096]{1,0:T(8,128)(2,1)}, u32[]{:S(2)}) copy-start(bf16[64,4096]{1,0:T(8,128)(2,1)} %refs_0_.1) | copy-start | bytes 1572868
  73.0 26.8 %collective-permute-start.4 = (bf16[48,4096]{1,0:T(8,128)(2,1)S(1)}, bf16[48,4096]{1,0:T(8,128)(2,1)S(1)}, u32[]{:S(2)}, u32[]{:S(2)}) collective-permute-start(bf16[48,4096]{1,0:T(8,128)(2,1)S(1)} %get-tuple-element.26), channel_id=1, source_target_pairs={{0,1},{1,0},{2,3},{3,2},{4,5},{5,4},{6,7},{7,6},{8,9},{9,8},{10,11... | collective-permute-start | bytes 1179656 | tf_op jit(solution)/shard_map/ppermute | solution.py:19
  77.3 47.3 %collective-permute-start.25 = (bf16[24,4096]{1,0:T(8,128)(2,1)S(1)}, bf16[24,4096]{1,0:T(8,128)(2,1)S(1)}, u32[]{:S(2)}, u32[]{:S(2)}) collective-permute-start(bf16[24,4096]{1,0:T(8,128)(2,1)S(1)} %get-tuple-element.39), channel_id=1, source_target_pairs={{0,2},{1,3},{2,0},{3,1},{4,6},{5,7},{6,4},{7,5},{8,10},{9,11},{10,... | collective-permute-start | bytes 589832 | tf_op jit(solution)/shard_map/ppermute | solution.py:19
  94.2 12.1 %collective-permute-start.12 = (bf16[24,4096]{1,0:T(8,128)(2,1)S(1)}, bf16[24,4096]{1,0:T(8,128)(2,1)S(1)}, u32[]{:S(2)}, u32[]{:S(2)}) collective-permute-start(bf16[24,4096]{1,0:T(8,128)(2,1)S(1)} %get-tuple-element.44), channel_id=1, source_target_pairs={{0,8},{1,9},{2,10},{3,11},{4,12},{5,13},{6,14},{7,15},{8,0},{9,1},... | collective-permute-start | bytes 589832 | tf_op jit(solution)/shard_map/ppermute | solution.py:19
  94.3 19.7 %collective-permute-start.13 = (bf16[24,4096]{1,0:T(8,128)(2,1)S(1)}, bf16[24,4096]{1,0:T(8,128)(2,1)S(1)}, u32[]{:S(2)}, u32[]{:S(2)}) collective-permute-start(bf16[24,4096]{1,0:T(8,128)(2,1)S(1)} %get-tuple-element.43), channel_id=1, source_target_pairs={{0,10},{1,11},{2,8},{3,9},{4,14},{5,15},{6,12},{7,13},{8,2},{9,3},... | collective-permute-start | bytes 589832 | tf_op jit(solution)/shard_map/ppermute | solution.py:19
  100.0 17.9 %collective-permute-start.5 = (bf16[24,4096]{1,0:T(8,128)(2,1)S(1)}, bf16[24,4096]{1,0:T(8,128)(2,1)S(1)}, u32[]{:S(2)}, u32[]{:S(2)}) collective-permute-start(bf16[24,4096]{1,0:T(8,128)(2,1)S(1)} %get-tuple-element.46), channel_id=1, source_target_pairs={{0,4},{1,5},{2,6},{3,7},{4,0},{5,1},{6,2},{7,3},{8,12},{9,13},{10,... | collective-permute-start | bytes 589832 | tf_op jit(solution)/shard_map/ppermute | solution.py:19
  100.1 24.1 %collective-permute-start.6 = (bf16[24,4096]{1,0:T(8,128)(2,1)S(1)}, bf16[24,4096]{1,0:T(8,128)(2,1)S(1)}, u32[]{:S(2)}, u32[]{:S(2)}) collective-permute-start(bf16[24,4096]{1,0:T(8,128)(2,1)S(1)} %get-tuple-element.45), channel_id=1, source_target_pairs={{0,6},{1,7},{2,4},{3,5},{4,2},{5,3},{6,0},{7,1},{8,14},{9,15},{10,... | collective-permute-start | bytes 589832 | tf_op jit(solution)/shard_map/ppermute | solution.py:19
  106.3 18.4 %collective-permute-start.19 = (bf16[24,4096]{1,0:T(8,128)(2,1)S(1)}, bf16[24,4096]{1,0:T(8,128)(2,1)S(1)}, u32[]{:S(2)}, u32[]{:S(2)}) collective-permute-start(bf16[24,4096]{1,0:T(8,128)(2,1)S(1)} %get-tuple-element.42), channel_id=1, source_target_pairs={{0,12},{1,13},{2,14},{3,15},{4,8},{5,9},{6,10},{7,11},{8,4},{9,5},... | collective-permute-start | bytes 589832 | tf_op jit(solution)/shard_map/ppermute | solution.py:19
  114.0 10.7 %collective-permute-start.20 = (bf16[24,4096]{1,0:T(8,128)(2,1)S(1)}, bf16[24,4096]{1,0:T(8,128)(2,1)S(1)}, u32[]{:S(2)}, u32[]{:S(2)}) collective-permute-start(bf16[24,4096]{1,0:T(8,128)(2,1)S(1)} %get-tuple-element.41), channel_id=1, source_target_pairs={{0,14},{1,15},{2,12},{3,13},{4,10},{5,11},{6,8},{7,9},{8,6},{9,7},... | collective-permute-start | bytes 589832 | tf_op jit(solution)/shard_map/ppermute | solution.py:19
